TPU v7x, 128 devices: a whole 4x4x4 slice. The times are simulated.
128 devices in a mesh: expert: 4 (over z), shard: 32 (over y, x, core).
Axes of the slice: x: 4, y: 4, z: 4, core: 2. Of those that a mesh axis runs over, the one named last changes fastest.
Arguments:
- master_gate: float32 [64, 2048, 1024], P('expert', 'shard'), may hold values from -0.25 to 0.25
- second_gate: float32 [64, 2048, 1024], P('expert', 'shard'), may hold values from -0.125 to 0.125
- master_up: float32 [64, 2048, 1024], P('expert', 'shard'), may hold values from -0.25 to 0.25
- second_up: float32 [64, 2048, 1024], P('expert', 'shard'), may hold values from -0.125 to 0.125
- mix_share: float32 [64], P('expert'), may hold values from 0.2 to 0.8
- router_weight: float32 [2048, 64], P('shard', 'expert'), may hold values from -0.125 to 0.125
- router_gain: float32 [2048], P('shard'), may hold values from 0.25 to 1.75
Outputs:
- final_gate: bfloat16 [64, 2048, 1024], P('expert', None, 'shard')
- final_up: bfloat16 [64, 2048, 1024], P('expert', None, 'shard')
- scale_gate: float32 [64, 1024], P('expert', 'shard')
- scale_up: float32 [64, 1024], P('expert', 'shard')
- serve_router: bfloat16 [2048, 64], replicated
All inputs are finite; a program needn't handle non-finite values.
Results may differ from a plain program's by a relative error of at most 0.001.
Values may be sent and summed in bfloat16 or wider, within the bound.
No kernel may reach another device: no remote copies, remote signals or barrier semaphores. Data moves between devices by JAX's collectives and lax.ppermute only.
A program may use at most 128 MiB of HBM per device.

v0:
```python
import jax
import jax.numpy as jnp
from jax import lax
from jax.experimental import pallas as pl
from jax.experimental.pallas import tpu as pltpu
from jax.sharding import PartitionSpec as P


D_MODEL = 2048
E, R, C, S = 16, 64, 1024, 32
W = C // S
PAIRS = E // 2
TP = 2 * PAIRS
MIB = 1024 * 1024
ORDER = [13, 3, 31, 6, 26, 27, 11, 25, 4, 18, 9, 17, 30, 0, 16, 15, 7, 12, 24, 1, 5, 23, 22, 28, 10, 20, 19, 8, 2, 21, 14, 29]
PLACE = [ORDER.index(s) for s in range(S)]


def lanes(shape):
    return lax.broadcasted_iota(jnp.int32, shape, 1)


def regroup(blocks):
    group = lanes((8, 128)) // W
    out = []
    for a in range(4):
        tile = blocks[0]
        for b in range(4):
            shift = ((b - a) * W) % 128
            moved = pltpu.roll(blocks[b], shift, 1) if shift else blocks[b]
            tile = moved if b == 0 else jnp.where(group == b, moved, tile)
        out.append(tile)
    return out


def join(first, second):
    return (
        jnp.concatenate([first[:, :64], second[:, :64]], axis=1),
        jnp.concatenate([first[:, 64:], second[:, 64:]], axis=1),
    )


def merge_kernel(mix, a_gate, b_gate, a_up, b_up, merged, sums, inputs, row_sums, sems):
    def copy(k, source, pair):
        return pltpu.make_async_copy(
            source.at[pl.ds(2 * pair, 2)], inputs.at[k, pl.ds(2 * pair, 2)], sems.at[k, pair]
        )

    sources = (a_gate, b_gate, a_up, b_up)
    for pair in range(PAIRS):
        for k, source in enumerate(sources):
            copy(k, source, pair).start()

    sublane = lax.broadcasted_iota(jnp.int32, (8, 128), 0)

    def step(pair, carry):
        for t in range(2):
            for k in (2 * t, 2 * t + 1):
                copy(k, sources[k], pair).wait()
            for par in range(2):
                e = 2 * pair + par
                share = mix[e]
                other = 1.0 - share
                for j in range(C // 128):
                    cols = slice(j * 128, (j + 1) * 128)
                    m = share * inputs[2 * t, e, :, cols] + other * inputs[2 * t + 1, e, :, cols]
                    merged[t * E + e, :, cols] = m
                    row_sums[t * 2 + pair // 4, :, cols] = jnp.where(
                        sublane == e % 8,
                        jnp.sum(jnp.abs(m), axis=0, keepdims=True),
                        row_sums[t * 2 + pair // 4, :, cols],
                    )
        return carry

    lax.fori_loop(0, PAIRS, step, 0)
    for j in range(C // 128):
        tiles = regroup([row_sums[g, :, j * 128 : (j + 1) * 128] for g in range(4)])
        for dd in range(4):
            sums[PLACE[j * 4 + dd]] = tiles[dd]


def scale_kernel(parts, spread, scale_gate, scale_up):
    scale = jnp.sum(parts[...], axis=0) / D_MODEL
    for s in range(S):
        spread[s] = scale
    for g in range(4):
        out = scale_gate if g < 2 else scale_up
        out[(g % 2) * 8 : (g % 2) * 8 + 8, :] = scale[:, g * W : (g + 1) * W]


def pack_kernel(merged, scales, gain, r0, r1, r2, r3, packed, inverse):
    for k, weight in enumerate((r0, r1, r2, r3)):
        served = weight[...] * gain[...]
        served = jnp.concatenate([served[:8], served[8:]], axis=1).astype(jnp.bfloat16)
        for d in range(S):
            packed[d, TP * W + 8 * k : TP * W + 8 * k + 8, :] = served
    for j in range(C // 128):
        tiles = regroup([scales[PLACE[4 * j + dd]] for dd in range(4)])
        for g in range(4):
            inverse[g, :, j * 128 : (j + 1) * 128] = 1.0 / tiles[g]

    for j in range(C // 128):
        cols = slice(j * 128, (j + 1) * 128)
        for tp in range(TP):
            halves = []
            for par in range(2):
                te = 2 * tp + par
                factor = inverse[te // 8, te % 8 : te % 8 + 1, cols]
                halves.append((merged[te, :, cols] * factor).astype(jnp.bfloat16))
            turned = jnp.concatenate(halves, axis=0).T
            for dd in range(4):
                rows = slice(tp * W, (tp + 1) * W)
                packed[PLACE[4 * j + dd], rows, :] = turned[dd * W : (dd + 1) * W]


def unpack_kernel(
    arrived, out_gate, out_up, out_router, joined, router, out_sems, router_sems
):
    me = lax.axis_index("expert")

    def serve(k):
        rows = pl.ds(pl.multiple_of(lax.rem(me + 4 - k, 4) * E, E), E)
        return pltpu.make_async_copy(router.at[k], out_router.at[rows], router_sems.at[k])

    def give(t, p):
        out = (out_gate, out_up)[t]
        return pltpu.make_async_copy(
            joined.at[t, pl.ds(2 * p, 2)], out.at[pl.ds(2 * p, 2)], out_sems.at[t, p]
        )

    def step(p, carry):
        for t in range(2):
            rows = pl.ds(pl.multiple_of((t * PAIRS + p) * W, W), W)
            for k in range(S // 2):
                cols = slice(k * 128, (k + 1) * 128)
                even, odd = join(arrived[PLACE[2 * k], rows], arrived[PLACE[2 * k + 1], rows])
                joined[t, 2 * p, :, cols] = even
                joined[t, 2 * p + 1, :, cols] = odd
            give(t, p).start()
        return carry

    lax.fori_loop(0, PAIRS, step, 0)
    for k in range(4):
        rows = slice(TP * W + 8 * k, TP * W + 8 * k + 8)
        for c in range(S // 2):
            low, high = join(arrived[PLACE[2 * c], rows], arrived[PLACE[2 * c + 1], rows])
            router[k, :8, c * 128 : (c + 1) * 128] = low
            router[k, 8:, c * 128 : (c + 1) * 128] = high
        serve(k).start()
    for p in range(PAIRS):
        for t in range(2):
            give(t, p).wait()
    for k in range(4):
        serve(k).wait()


def whole():
    return pl.BlockSpec(memory_space=pltpu.VMEM)


def remote():
    return pl.BlockSpec(memory_space=pltpu.HBM)


def params(mib):
    return pltpu.CompilerParams(vmem_limit_bytes=mib * MIB)


def exchange(x):
    return lax.all_to_all(
        x, "shard", split_axis=0, concat_axis=0, tiled=True, axis_index_groups=[ORDER]
    )


def serve_step(master_gate, second_gate, master_up, second_up, mix_share, router_weight, router_gain):
    weight = router_weight.T
    hops = [
        lax.ppermute(weight, "expert", [(z, (z + k) % 4) for z in range(4)])
        for k in range(1, 4)
    ]

    merged, sums = pl.pallas_call(
        merge_kernel,
        in_specs=[pl.BlockSpec(memory_space=pltpu.SMEM)] + [remote()] * 4,
        out_specs=[whole(), whole()],
        out_shape=[
            pltpu.VMEM((2 * E, R, C), jnp.float32),
            pltpu.VMEM((S, 8, 128), jnp.float32),
        ],
        scratch_shapes=[
            pltpu.VMEM((4, E, R, C), jnp.float32),
            pltpu.VMEM((4, 8, C), jnp.float32),
            pltpu.SemaphoreType.DMA((4, PAIRS)),
        ],
        compiler_params=params(20),
        name="merge",
    )(
        *(
            pltpu.with_memory_space_constraint(x, pltpu.HBM)
            for x in (mix_share, master_gate, second_gate, master_up, second_up)
        ),
    )

    parts = exchange(sums)

    spread, scale_gate, scale_up = pl.pallas_call(
        scale_kernel,
        in_specs=[whole()],
        out_specs=[whole()] * 3,
        out_shape=[
            jax.ShapeDtypeStruct((S, 8, 128), jnp.float32),
            jax.ShapeDtypeStruct((E, W), jnp.float32),
            jax.ShapeDtypeStruct((E, W), jnp.float32),
        ],
        compiler_params=params(4),
        name="scale",
    )(parts)
    scales = exchange(spread)

    rows = TP * W + 4 * E // 2
    packed = pl.pallas_call(
        pack_kernel,
        in_specs=[whole()] * 7,
        out_specs=whole(),
        out_shape=pltpu.VMEM((S, rows, 128), jnp.bfloat16),
        scratch_shapes=[pltpu.VMEM((4, 8, C), jnp.float32)],
        compiler_params=params(4),
        name="pack",
    )(merged, scales, router_gain[None, :], weight, *hops)
    arrived = pltpu.with_memory_space_constraint(exchange(packed), pltpu.VMEM)

    final_gate, final_up, serve_router = pl.pallas_call(
        unpack_kernel,
        in_specs=[whole()],
        out_specs=[remote()] * 3,
        out_shape=[jax.ShapeDtypeStruct((E, W, S * R), jnp.bfloat16)] * 2
        + [jax.ShapeDtypeStruct((4 * E, S * R), jnp.bfloat16)],
        scratch_shapes=[
            pltpu.VMEM((2, E, W, S * R), jnp.bfloat16),
            pltpu.VMEM((4, E, S * R), jnp.bfloat16),
            pltpu.SemaphoreType.DMA((2, PAIRS)),
            pltpu.SemaphoreType.DMA((4,)),
        ],
        compiler_params=params(10),
        name="unpack",
    )(arrived)
    return (
        final_gate.transpose(0, 2, 1),
        final_up.transpose(0, 2, 1),
        scale_gate,
        scale_up,
        serve_router.T,
    )


def solution(mesh):
    in_specs = (
        P("expert", "shard", None),
        P("expert", "shard", None),
        P("expert", "shard", None),
        P("expert", "shard", None),
        P("expert"),
        P("shard", "expert"),
        P("shard"),
    )
    out_specs = (
        P("expert", None, "shard"),
        P("expert", None, "shard"),
        P("expert", "shard"),
        P("expert", "shard"),
        P(),
    )
    return jax.shard_map(serve_step, mesh=mesh, in_specs=in_specs, out_specs=out_specs, check_vma=False)
```

profile of v0, /device:TPU:0, one launch (start us, length us, event | category | flops | bytes accessed | tf_op | source)
XLA Modules:
  0.0 105.1 jit_solution(4078779974399527972)
XLA Ops:
  0.6 0.0 copy-start.2
  0.6 0.0 copy-start.3
  0.7 7.1 %merge.1 = (f32[32,64,1024]{2,1,0:T(8,128)S(1)}, f32[32,8,128]{2,1,0:T(8,128)S(1)}) custom-call(f32[16]{0:T(128)} %mix.1, f32[16,64,1024]{2,1,0:T(8,128)} %a_gate.1, f32[16,64,1024]{2,1,0:T(8,128)} %b_gate.1, f32[16,64,1024]{2,1,0:T(8,128)} %a_up.1, f32[16,64,1024]{2,1,0:T(8,128)} %b_up.1), custom_call_target="tpu_custom_call" | custom-call | tf_op jit(solution)/shard_map/merge/pallas_call | solution.py:182
  7.8 0.0 copy-start
  7.8 3.2 %copy-done = f32[32,64,1024]{2,1,0:T(8,128)} copy-done((f32[32,64,1024]{2,1,0:T(8,128)}, f32[32,64,1024]{2,1,0:T(8,128)S(1)}, u32[]{:S(2)}) %copy-start) | copy-done | bytes 8388632
  11.0 12.8 %all_to_all.15.parts = f32[32,8,128]{2,1,0:T(8,128)S(1)} all-to-all(f32[32,8,128]{2,1,0:T(8,128)S(1)} %get-tuple-element.14), channel_id=1, replica_groups={{13,3,31,6,26,27,11,25,4,18,9,17,30,0,16,15,7,12,24,1,5,23,22,28,10,20,..., dimensions={0} | all-to-all | bytes 262144 | tf_op jit(solution)/shard_map/all_to_all | solution.py:170
  23.8 0.7 scale.1
  24.5 6.1 %all-to-all-start.1 = ((f32[32,8,128]{2,1,0:T(8,128)}), f32[32,8,128]{2,1,0:T(8,128)S(1)}, u32[]{:S(2)}, u32[]{:S(2)}) async-start(f32[32,8,128]{2,1,0:T(8,128)} %get-tuple-element.15), calls=%async_computation.1 | async-start | bytes 262144 | tf_op jit(solution)/shard_map/all_to_all | solution.py:170
  30.6 0.0 copy-done.2
  30.6 4.1 %collective-permute-start.2 = (f32[16,64]{1,0:T(8,128)S(1)}, f32[16,64]{1,0:T(8,128)S(1)}, u32[]{:S(2)}, u32[]{:S(2)}) collective-permute-start(f32[16,64]{1,0:T(8,128)S(1)} %bitcast.5), channel_id=1, source_target_pairs={{0,96},{32,0},{64,32},{96,64},{1,97},{33,1},{65,33},{97,65},{2,98}... | collective-permute-start | bytes 12296 | tf_op jit(solution)/shard_map/ppermute | solution.py:178
  34.7 0.0 collective-permute-start.1
  34.7 1.3 %collective-permute-start = (f32[16,64]{1,0:T(8,128)S(1)}, f32[16,64]{1,0:T(8,128)S(1)}, u32[]{:S(2)}, u32[]{:S(2)}) collective-permute-start(f32[16,64]{1,0:T(8,128)S(1)} %bitcast.7), channel_id=1, source_target_pairs={{0,32},{32,64},{64,96},{96,0},{1,33},{33,65},{65,97},{97,1},{2,34}... | collective-permute-start | bytes 12296 | tf_op jit(solution)/shard_map/ppermute | solution.py:178
  36.0 0.1 collective-permute-done.2.r3
  36.1 3.8 %collective-permute-done.1.r2 = f32[16,64]{1,0:T(8,128)S(1)} collective-permute-done((f32[16,64]{1,0:T(8,128)S(1)}, f32[16,64]{1,0:T(8,128)S(1)}, u32[]{:S(2)}, u32[]{:S(2)}) %collective-permute-start.1) | collective-permute-done | bytes 4128 | tf_op jit(solution)/shard_map/ppermute | solution.py:178
  39.9 0.0 collective-permute-done.r1
  39.9 0.0 all-to-all-done.1.scales
  39.9 0.0 copy-done.3
  39.9 0.0 copy-start.1
  39.9 3.4 %copy-done.1 = f32[32,64,1024]{2,1,0:T(8,128)S(1)} copy-done((f32[32,64,1024]{2,1,0:T(8,128)S(1)}, f32[32,64,1024]{2,1,0:T(8,128)}, u32[]{:S(2)}) %copy-start.1) | copy-done | bytes 8388632
  43.3 1.3 %pack.1 = bf16[32,544,128]{2,1,0:T(8,128)(2,1)S(1)} custom-call(f32[32,64,1024]{2,1,0:T(8,128)S(1)} %copy-done.1, f32[32,8,128]{2,1,0:T(8,128)S(1)} %all-to-all-done.1.scales, f32[1,64]{1,0:T(1,128)S(1)} %bitcast.9, f32[16,64]{1,0:T(8,128)S(1)} %bitcast.8, f32[16,64]{1,0:T(8,128)S(1)} %collective-permute-done.r1, f32[16,64]{1,0:T(8,128)S(1)} %collective-permute-done.1.r2, ...), custom_call_target="tpu_custom_call" | custom-call | tf_op jit(solution)/shard_map/pack/pallas_call | solution.py:221
  44.6 57.9 %all_to_all.16.arrived = bf16[32,544,128]{2,1,0:T(8,128)(2,1)S(1)} all-to-all(bf16[32,544,128]{2,1,0:T(8,128)(2,1)S(1)} %pack.1), channel_id=1, replica_groups={{13,3,31,6,26,27,11,25,4,18,9,17,30,0,16,15,7,12,24,1,5,23,22,28,10,20,..., dimensions={0} | all-to-all | bytes 8912896 | tf_op jit(solution)/shard_map/all_to_all | solution.py:170
  102.5 2.6 %unpack.1 = (bf16[16,32,2048]{2,1,0:T(8,128)(2,1)}, bf16[16,32,2048]{2,1,0:T(8,128)(2,1)}, bf16[64,2048]{1,0:T(8,128)(2,1)}) custom-call(bf16[32,544,128]{2,1,0:T(8,128)(2,1)S(1)} %all_to_all.16.arrived), custom_call_target="tpu_custom_call" | custom-call | tf_op jit(solution)/shard_map/unpack/pallas_call | solution.py:232
Async XLA Ops:
  0.6 30.0 %copy-start.2 = (f32[64,16]{0,1:T(8,128)S(1)}, f32[64,16]{0,1:T(8,128)}, u32[]{:S(2)}) copy-start(f32[64,16]{0,1:T(8,128)} %param.12) | copy-start | bytes 12292
  0.6 39.3 %copy-start.3 = (f32[64]{0:T(128)S(1)}, f32[64]{0:T(128)}, u32[]{:S(2)}) copy-start(f32[64]{0:T(128)} %param.13) | copy-start | bytes 772
  7.8 3.2 %copy-start = (f32[32,64,1024]{2,1,0:T(8,128)}, f32[32,64,1024]{2,1,0:T(8,128)S(1)}, u32[]{:S(2)}) copy-start(f32[32,64,1024]{2,1,0:T(8,128)S(1)} %get-tuple-element.13.merged) | copy-start | bytes 25165828
  24.5 15.4 %all-to-all-start.1 = ((f32[32,8,128]{2,1,0:T(8,128)}), f32[32,8,128]{2,1,0:T(8,128)S(1)}, u32[]{:S(2)}, u32[]{:S(2)}) async-start(f32[32,8,128]{2,1,0:T(8,128)} %get-tuple-element.15), calls=%async_computation.1 | async-start | bytes 262144 | tf_op jit(solution)/shard_map/all_to_all | solution.py:170
  30.6 5.5 %collective-permute-start.2 = (f32[16,64]{1,0:T(8,128)S(1)}, f32[16,64]{1,0:T(8,128)S(1)}, u32[]{:S(2)}, u32[]{:S(2)}) collective-permute-start(f32[16,64]{1,0:T(8,128)S(1)} %bitcast.5), channel_id=1, source_target_pairs={{0,96},{32,0},{64,32},{96,64},{1,97},{33,1},{65,33},{97,65},{2,98}... | collective-permute-start | bytes 12296 | tf_op jit(solution)/shard_map/ppermute | solution.py:178
  34.7 5.2 %collective-permute-start.1 = (f32[16,64]{1,0:T(8,128)S(1)}, f32[16,64]{1,0:T(8,128)S(1)}, u32[]{:S(2)}, u32[]{:S(2)}) collective-permute-start(f32[16,64]{1,0:T(8,128)S(1)} %bitcast.6), channel_id=1, source_target_pairs={{0,64},{32,96},{64,0},{96,32},{1,65},{33,97},{65,1},{97,33},{2,66}... | collective-permute-start | bytes 12296 | tf_op jit(solution)/shard_map/ppermute | solution.py:178
  34.7 5.2 %collective-permute-start = (f32[16,64]{1,0:T(8,128)S(1)}, f32[16,64]{1,0:T(8,128)S(1)}, u32[]{:S(2)}, u32[]{:S(2)}) collective-permute-start(f32[16,64]{1,0:T(8,128)S(1)} %bitcast.7), channel_id=1, source_target_pairs={{0,32},{32,64},{64,96},{96,0},{1,33},{33,65},{65,97},{97,1},{2,34}... | collective-permute-start | bytes 12296 | tf_op jit(solution)/shard_map/ppermute | solution.py:178
  39.9 3.4 %copy-start.1 = (f32[32,64,1024]{2,1,0:T(8,128)S(1)}, f32[32,64,1024]{2,1,0:T(8,128)}, u32[]{:S(2)}) copy-start(f32[32,64,1024]{2,1,0:T(8,128)} %copy-done) | copy-start | bytes 25165828
where the time goes:
time: 106 us; the launch traced here: 105 us
  blocking collectives  70.6 us (67%)
  Pallas kernels  11.8 us (11%)
  starting transfers between devices  11.5 us (11%)
  local copies, waits for them, and re-layouts  6.59 us (6%)
  waiting for transfers between devices  3.9 us (4%)
    all_to_all x2, blocking collectives, exchange(): lax.all_to_all(x, 'shard', split_axis=0, concat_axis=0, tiled=True, axis_...  70.6 us
    pallas_call x1, Pallas kernels, serve_step(): pl.pallas_call(merge_kernel, in_specs=[pl.BlockSpec(memory_space=pltpu.SM...  7.12 us
    unnamed x8, local copies, waits for them, and re-layouts  6.59 us
    all_to_all x1, starting transfers between devices, exchange(): lax.all_to_all(x, 'shard', split_axis=0, concat_axis=0, tiled=True, axis_...  6.15 us
    ppermute x3, starting transfers between devices, serve_step(): lax.ppermute(weight, 'expert', [(z, (z + k) % 4) for z in range(4)])  5.37 us
    ppermute x3, waiting for transfers between devices, serve_step(): lax.ppermute(weight, 'expert', [(z, (z + k) % 4) for z in range(4)])  3.9 us
    pallas_call x1, Pallas kernels, serve_step(): pl.pallas_call(unpack_kernel, in_specs=[whole()], out_specs=[remote()] *...  2.64 us
  transfers between devices with their start and end apart: 4, of which 2 were waited for; matrix products, arithmetic and copies ran while one was open for 0% of the time, Pallas kernels for 0%

commit v1 on v0

--- a/solution.py
+++ b/solution.py
@@ -40,7 +40,9 @@
     )
 
 
-def merge_kernel(mix, a_gate, b_gate, a_up, b_up, merged, sums, inputs, row_sums, sems):
+def merge_kernel(
+    mix, a_gate, b_gate, a_up, b_up, router, gain, merged, sums, inputs, row_sums, sems
+):
     def copy(k, source, pair):
         return pltpu.make_async_copy(
             source.at[pl.ds(2 * pair, 2)], inputs.at[k, pl.ds(2 * pair, 2)], sems.at[k, pair]
@@ -51,6 +53,10 @@
         for k, source in enumerate(sources):
             copy(k, source, pair).start()
 
+    served = router[...] * gain[...]
+    served = jnp.concatenate([served[:8], served[8:]], axis=1)
+    for s in range(S):
+        sums[s, 8:, :] = served
     sublane = lax.broadcasted_iota(jnp.int32, (8, 128), 0)
 
     def step(pair, carry):
@@ -76,11 +82,16 @@
     for j in range(C // 128):
         tiles = regroup([row_sums[g, :, j * 128 : (j + 1) * 128] for g in range(4)])
         for dd in range(4):
-            sums[PLACE[j * 4 + dd]] = tiles[dd]
-
-
-def scale_kernel(parts, spread, scale_gate, scale_up):
-    scale = jnp.sum(parts[...], axis=0) / D_MODEL
+            sums[PLACE[j * 4 + dd], :8, :] = tiles[dd]
+
+
+def scale_kernel(parts, spread, router, scale_gate, scale_up):
+    scale = jnp.sum(parts[:, :8, :], axis=0) / D_MODEL
+    for k in range(S // 2):
+        low, high = join(parts[PLACE[2 * k], 8:, :], parts[PLACE[2 * k + 1], 8:, :])
+        router[:, k * 128 : (k + 1) * 128] = jnp.concatenate([low, high], axis=0).astype(
+            jnp.bfloat16
+        )
     for s in range(S):
         spread[s] = scale
     for g in range(4):
@@ -88,12 +99,7 @@
         out[(g % 2) * 8 : (g % 2) * 8 + 8, :] = scale[:, g * W : (g + 1) * W]
 
 
-def pack_kernel(merged, scales, gain, r0, r1, r2, r3, packed, inverse):
-    for k, weight in enumerate((r0, r1, r2, r3)):
-        served = weight[...] * gain[...]
-        served = jnp.concatenate([served[:8], served[8:]], axis=1).astype(jnp.bfloat16)
-        for d in range(S):
-            packed[d, TP * W + 8 * k : TP * W + 8 * k + 8, :] = served
+def pack_kernel(merged, scales, packed, inverse):
     for j in range(C // 128):
         tiles = regroup([scales[PLACE[4 * j + dd]] for dd in range(4)])
         for g in range(4):
@@ -114,13 +120,14 @@
 
 
 def unpack_kernel(
-    arrived, out_gate, out_up, out_router, joined, router, out_sems, router_sems
+    arrived, r0, r1, r2, r3, out_gate, out_up, out_router, joined, out_sems, router_sems
 ):
     me = lax.axis_index("expert")
+    routers = (r0, r1, r2, r3)
 
     def serve(k):
         rows = pl.ds(pl.multiple_of(lax.rem(me + 4 - k, 4) * E, E), E)
-        return pltpu.make_async_copy(router.at[k], out_router.at[rows], router_sems.at[k])
+        return pltpu.make_async_copy(routers[k], out_router.at[rows], router_sems.at[k])
 
     def give(t, p):
         out = (out_gate, out_up)[t]
@@ -139,14 +146,9 @@
             give(t, p).start()
         return carry
 
+    for k in range(4):
+        serve(k).start()
     lax.fori_loop(0, PAIRS, step, 0)
-    for k in range(4):
-        rows = slice(TP * W + 8 * k, TP * W + 8 * k + 8)
-        for c in range(S // 2):
-            low, high = join(arrived[PLACE[2 * c], rows], arrived[PLACE[2 * c + 1], rows])
-            router[k, :8, c * 128 : (c + 1) * 128] = low
-            router[k, 8:, c * 128 : (c + 1) * 128] = high
-        serve(k).start()
     for p in range(PAIRS):
         for t in range(2):
             give(t, p).wait()
@@ -173,19 +175,13 @@
 
 
 def serve_step(master_gate, second_gate, master_up, second_up, mix_share, router_weight, router_gain):
-    weight = router_weight.T
-    hops = [
-        lax.ppermute(weight, "expert", [(z, (z + k) % 4) for z in range(4)])
-        for k in range(1, 4)
-    ]
-
     merged, sums = pl.pallas_call(
         merge_kernel,
-        in_specs=[pl.BlockSpec(memory_space=pltpu.SMEM)] + [remote()] * 4,
+        in_specs=[pl.BlockSpec(memory_space=pltpu.SMEM)] + [remote()] * 4 + [whole()] * 2,
         out_specs=[whole(), whole()],
         out_shape=[
             pltpu.VMEM((2 * E, R, C), jnp.float32),
-            pltpu.VMEM((S, 8, 128), jnp.float32),
+            pltpu.VMEM((S, 16, 128), jnp.float32),
         ],
         scratch_shapes=[
             pltpu.VMEM((4, E, R, C), jnp.float32),
@@ -199,51 +195,56 @@
             pltpu.with_memory_space_constraint(x, pltpu.HBM)
             for x in (mix_share, master_gate, second_gate, master_up, second_up)
         ),
+        pltpu.with_memory_space_constraint(router_weight.T, pltpu.HBM),
+        pltpu.with_memory_space_constraint(router_gain[None, :], pltpu.HBM),
     )
 
     parts = exchange(sums)
 
-    spread, scale_gate, scale_up = pl.pallas_call(
+    spread, router, scale_gate, scale_up = pl.pallas_call(
         scale_kernel,
         in_specs=[whole()],
-        out_specs=[whole()] * 3,
+        out_specs=[whole()] * 4,
         out_shape=[
-            jax.ShapeDtypeStruct((S, 8, 128), jnp.float32),
+            pltpu.VMEM((S, 8, 128), jnp.float32),
+            pltpu.VMEM((E, S * R), jnp.bfloat16),
             jax.ShapeDtypeStruct((E, W), jnp.float32),
             jax.ShapeDtypeStruct((E, W), jnp.float32),
         ],
         compiler_params=params(4),
         name="scale",
     )(parts)
+    hops = [
+        lax.ppermute(router, "expert", [(z, (z + k) % 4) for z in range(4)])
+        for k in range(1, 4)
+    ]
     scales = exchange(spread)
 
-    rows = TP * W + 4 * E // 2
     packed = pl.pallas_call(
         pack_kernel,
-        in_specs=[whole()] * 7,
+        in_specs=[whole()] * 2,
         out_specs=whole(),
-        out_shape=pltpu.VMEM((S, rows, 128), jnp.bfloat16),
+        out_shape=pltpu.VMEM((S, TP * W, 128), jnp.bfloat16),
         scratch_shapes=[pltpu.VMEM((4, 8, C), jnp.float32)],
         compiler_params=params(4),
         name="pack",
-    )(merged, scales, router_gain[None, :], weight, *hops)
+    )(merged, scales)
     arrived = pltpu.with_memory_space_constraint(exchange(packed), pltpu.VMEM)
 
     final_gate, final_up, serve_router = pl.pallas_call(
         unpack_kernel,
-        in_specs=[whole()],
+        in_specs=[whole()] * 5,
         out_specs=[remote()] * 3,
         out_shape=[jax.ShapeDtypeStruct((E, W, S * R), jnp.bfloat16)] * 2
         + [jax.ShapeDtypeStruct((4 * E, S * R), jnp.bfloat16)],
         scratch_shapes=[
             pltpu.VMEM((2, E, W, S * R), jnp.bfloat16),
-            pltpu.VMEM((4, E, S * R), jnp.bfloat16),
             pltpu.SemaphoreType.DMA((2, PAIRS)),
             pltpu.SemaphoreType.DMA((4,)),
         ],
         compiler_params=params(10),
         name="unpack",
-    )(arrived)
+    )(arrived, router, *hops)
     return (
         final_gate.transpose(0, 2, 1),
         final_up.transpose(0, 2, 1),

time: 106 us -> 105 us (level)
  the two profiles are of different devices: /device:TPU:0 before, /device:TPU:34 now
where the time goes in v1:
time: 105 us
  waiting for transfers between devices  53.2 us (51%)
  blocking collectives  24.4 us (23%)
  Pallas kernels  13.7 us (13%)
  starting transfers between devices  11.2 us (11%)
  local copies, waits for them, and re-layouts  1.97 us (2%)
    all_to_all x1, waiting for transfers between devices, exchange(): lax.all_to_all(x, 'shard', split_axis=0, concat_axis=0, tiled=True, axis_...  51.1 us
    all_to_all x2, blocking collectives, exchange(): lax.all_to_all(x, 'shard', split_axis=0, concat_axis=0, tiled=True, axis_...  24.4 us
    pallas_call x1, Pallas kernels, serve_step(): pl.pallas_call(merge_kernel, in_specs=[pl.BlockSpec(memory_space=pltpu.SM...  7.04 us
    ppermute x3, starting transfers between devices, serve_step(): lax.ppermute(router, 'expert', [(z, (z + k) % 4) for z in range(4)])  5.68 us
    all_to_all x1, starting transfers between devices, exchange(): lax.all_to_all(x, 'shard', split_axis=0, concat_axis=0, tiled=True, axis_...  5.54 us
    pallas_call x1, Pallas kernels, serve_step(): pl.pallas_call(unpack_kernel, in_specs=[whole()] * 5, out_specs=[remote()...  4.73 us
  transfers between devices with their start and end apart: 4, of which 3 were waited for; matrix products, arithmetic and copies ran while one was open for 0% of the time, Pallas kernels for 0%

profile of v1, /device:TPU:34, one launch (start us, length us, event | category | flops | bytes accessed | tf_op | source)
XLA Modules:
  0.0 105.2 jit_solution(4681776333775655951)
XLA Ops:
  0.6 7.0 %merge.1 = (f32[32,64,1024]{2,1,0:T(8,128)S(1)}, f32[32,16,128]{2,1,0:T(8,128)S(1)}) custom-call(f32[16]{0:T(128)} %mix.1, f32[16,64,1024]{2,1,0:T(8,128)} %a_gate.1, f32[16,64,1024]{2,1,0:T(8,128)} %b_gate.1, f32[16,64,1024]{2,1,0:T(8,128)} %a_up.1, f32[16,64,1024]{2,1,0:T(8,128)} %b_up.1, f32[16,64]{1,0:T(8,128)} %bitcast.5, f32[1,64]{1,0:T(1,128)} %bitcast.6), custom_call_target="tpu_custom_call" | custom-call | tf_op jit(solution)/shard_map/merge/pallas_call | solution.py:178
  7.7 14.0 %all_to_all.15.parts = f32[32,16,128]{2,1,0:T(8,128)S(1)} all-to-all(f32[32,16,128]{2,1,0:T(8,128)S(1)} %get-tuple-element.15), channel_id=1, replica_groups={{13,3,31,6,26,27,11,25,4,18,9,17,30,0,16,15,7,12,24,1,5,23,22,28,10,20,..., dimensions={0} | all-to-all | bytes 524288 | tf_op jit(solution)/shard_map/all_to_all | solution.py:172
  21.7 0.7 scale.1
  22.4 10.4 %all_to_all.16.scales = f32[32,8,128]{2,1,0:T(8,128)S(1)} all-to-all(f32[32,8,128]{2,1,0:T(8,128)S(1)} %get-tuple-element.16), channel_id=1, replica_groups={{13,3,31,6,26,27,11,25,4,18,9,17,30,0,16,15,7,12,24,1,5,23,22,28,10,20,..., dimensions={0} | all-to-all | bytes 262144 | tf_op jit(solution)/shard_map/all_to_all | solution.py:172
  32.8 1.3 %pack.1 = bf16[32,512,128]{2,1,0:T(8,128)(2,1)S(1)} custom-call(f32[32,64,1024]{2,1,0:T(8,128)S(1)} %get-tuple-element.14.merged, f32[32,8,128]{2,1,0:T(8,128)S(1)} %all_to_all.16.scales), custom_call_target="tpu_custom_call" | custom-call | tf_op jit(solution)/shard_map/pack/pallas_call | solution.py:223
  34.1 0.0 copy-start
  34.1 2.0 %copy-done = bf16[32,512,128]{2,1,0:T(8,128)(2,1)} copy-done((bf16[32,512,128]{2,1,0:T(8,128)(2,1)}, bf16[32,512,128]{2,1,0:T(8,128)(2,1)S(1)}, u32[]{:S(2)}) %copy-start) | copy-done | bytes 4194328
  36.1 5.5 %all-to-all-start.2 = ((bf16[32,512,128]{2,1,0:T(8,128)(2,1)}), bf16[32,512,128]{2,1,0:T(8,128)(2,1)}, u32[]{:S(2)}, u32[]{:S(2)}) async-start(bf16[32,512,128]{2,1,0:T(8,128)(2,1)} %copy-done), calls=%async_computation.2 | async-start | bytes 8388608 | tf_op jit(solution)/shard_map/all_to_all | solution.py:172
  41.6 0.2 collective-permute-start.2
  41.8 3.3 %collective-permute-start.1 = (bf16[16,2048]{1,0:T(8,128)(2,1)S(1)}, bf16[16,2048]{1,0:T(8,128)(2,1)S(1)}, u32[]{:S(2)}, u32[]{:S(2)}) collective-permute-start(bf16[16,2048]{1,0:T(8,128)(2,1)S(1)} %get-tuple-element.17.r0), channel_id=1, source_target_pairs={{0,64},{32,96},{64,0},{96,32},{1,65},{33,97},{65,1},{97,33},{2,66}... | collective-permute-start | bytes 196616 | tf_op jit(solution)/shard_map/ppermute | solution.py:218
  45.1 2.2 %collective-permute-start = (bf16[16,2048]{1,0:T(8,128)(2,1)S(1)}, bf16[16,2048]{1,0:T(8,128)(2,1)S(1)}, u32[]{:S(2)}, u32[]{:S(2)}) collective-permute-start(bf16[16,2048]{1,0:T(8,128)(2,1)S(1)} %get-tuple-element.17.r0), channel_id=1, source_target_pairs={{0,32},{32,64},{64,96},{96,0},{1,33},{33,65},{65,97},{97,1},{2,34}... | collective-permute-start | bytes 196616 | tf_op jit(solution)/shard_map/ppermute | solution.py:218
  47.3 0.0 collective-permute-done.2.r3
  47.3 1.1 %collective-permute-done.1.r2 = bf16[16,2048]{1,0:T(8,128)(2,1)S(1)} collective-permute-done((bf16[16,2048]{1,0:T(8,128)(2,1)S(1)}, bf16[16,2048]{1,0:T(8,128)(2,1)S(1)}, u32[]{:S(2)}, u32[]{:S(2)}) %collective-permute-start.1) | collective-permute-done | bytes 65568 | tf_op jit(solution)/shard_map/ppermute | solution.py:218
  48.4 1.0 collective-permute-done.r1
  49.3 51.1 %all-to-all-done.2.arrived = bf16[32,512,128]{2,1,0:T(8,128)(2,1)} async-done(((bf16[32,512,128]{2,1,0:T(8,128)(2,1)}), bf16[32,512,128]{2,1,0:T(8,128)(2,1)}, u32[]{:S(2)}, u32[]{:S(2)}) %all-to-all-start.2) | async-done | bytes 4194336 | tf_op jit(solution)/shard_map/all_to_all | solution.py:172
  100.4 4.7 %unpack.1 = (bf16[16,32,2048]{2,1,0:T(8,128)(2,1)}, bf16[16,32,2048]{2,1,0:T(8,128)(2,1)}, bf16[64,2048]{1,0:T(8,128)(2,1)}) custom-call(bf16[32,512,128]{2,1,0:T(8,128)(2,1)} %all-to-all-done.2.arrived, bf16[16,2048]{1,0:T(8,128)(2,1)S(1)} %get-tuple-element.17.r0, bf16[16,2048]{1,0:T(8,128)(2,1)S(1)} %collective-permute-done.r1, ...), custom_call_target="tpu_custom_call" | custom-call | tf_op jit(solution)/shard_map/unpack/pallas_call | solution.py:234
Async XLA Ops:
  34.1 2.0 %copy-start = (bf16[32,512,128]{2,1,0:T(8,128)(2,1)}, bf16[32,512,128]{2,1,0:T(8,128)(2,1)S(1)}, u32[]{:S(2)}) copy-start(bf16[32,512,128]{2,1,0:T(8,128)(2,1)S(1)} %pack.1) | copy-start | bytes 12582916
  36.1 64.4 %all-to-all-start.2 = ((bf16[32,512,128]{2,1,0:T(8,128)(2,1)}), bf16[32,512,128]{2,1,0:T(8,128)(2,1)}, u32[]{:S(2)}, u32[]{:S(2)}) async-start(bf16[32,512,128]{2,1,0:T(8,128)(2,1)} %copy-done), calls=%async_computation.2 | async-start | bytes 8388608 | tf_op jit(solution)/shard_map/all_to_all | solution.py:172
  41.6 5.7 %collective-permute-start.2 = (bf16[16,2048]{1,0:T(8,128)(2,1)S(1)}, bf16[16,2048]{1,0:T(8,128)(2,1)S(1)}, u32[]{:S(2)}, u32[]{:S(2)}) collective-permute-start(bf16[16,2048]{1,0:T(8,128)(2,1)S(1)} %get-tuple-element.17.r0), channel_id=1, source_target_pairs={{0,96},{32,0},{64,32},{96,64},{1,97},{33,1},{65,33},{97,65},{2,98}... | collective-permute-start | bytes 196616 | tf_op jit(solution)/shard_map/ppermute | solution.py:218
  41.8 6.6 %collective-permute-start.1 = (bf16[16,2048]{1,0:T(8,128)(2,1)S(1)}, bf16[16,2048]{1,0:T(8,128)(2,1)S(1)}, u32[]{:S(2)}, u32[]{:S(2)}) collective-permute-start(bf16[16,2048]{1,0:T(8,128)(2,1)S(1)} %get-tuple-element.17.r0), channel_id=1, source_target_pairs={{0,64},{32,96},{64,0},{96,32},{1,65},{33,97},{65,1},{97,33},{2,66}... | collective-permute-start | bytes 196616 | tf_op jit(solution)/shard_map/ppermute | solution.py:218
  45.1 4.3 %collective-permute-start = (bf16[16,2048]{1,0:T(8,128)(2,1)S(1)}, bf16[16,2048]{1,0:T(8,128)(2,1)S(1)}, u32[]{:S(2)}, u32[]{:S(2)}) collective-permute-start(bf16[16,2048]{1,0:T(8,128)(2,1)S(1)} %get-tuple-element.17.r0), channel_id=1, source_target_pairs={{0,32},{32,64},{64,96},{96,0},{1,33},{33,65},{65,97},{97,1},{2,34}... | collective-permute-start | bytes 196616 | tf_op jit(solution)/shard_map/ppermute | solution.py:218

commit v2 on v1

--- a/solution.py
+++ b/solution.py
@@ -54,9 +54,9 @@
             copy(k, source, pair).start()
 
     served = router[...] * gain[...]
-    served = jnp.concatenate([served[:8], served[8:]], axis=1)
+    served = jnp.concatenate([served[:8], served[8:]], axis=1).astype(jnp.bfloat16)
     for s in range(S):
-        sums[s, 8:, :] = served
+        sums[s, 16:, :] = served
     sublane = lax.broadcasted_iota(jnp.int32, (8, 128), 0)
 
     def step(pair, carry):
@@ -82,16 +82,18 @@
     for j in range(C // 128):
         tiles = regroup([row_sums[g, :, j * 128 : (j + 1) * 128] for g in range(4)])
         for dd in range(4):
-            sums[PLACE[j * 4 + dd], :8, :] = tiles[dd]
+            high = tiles[dd].astype(jnp.bfloat16)
+            rest = (tiles[dd] - high.astype(jnp.float32)).astype(jnp.bfloat16)
+            sums[PLACE[j * 4 + dd], :8, :] = high
+            sums[PLACE[j * 4 + dd], 8:16, :] = rest
 
 
 def scale_kernel(parts, spread, router, scale_gate, scale_up):
-    scale = jnp.sum(parts[:, :8, :], axis=0) / D_MODEL
+    both = parts[:, :8, :].astype(jnp.float32) + parts[:, 8:16, :].astype(jnp.float32)
+    scale = jnp.sum(both, axis=0) / D_MODEL
     for k in range(S // 2):
-        low, high = join(parts[PLACE[2 * k], 8:, :], parts[PLACE[2 * k + 1], 8:, :])
-        router[:, k * 128 : (k + 1) * 128] = jnp.concatenate([low, high], axis=0).astype(
-            jnp.bfloat16
-        )
+        low, high = join(parts[PLACE[2 * k], 16:, :], parts[PLACE[2 * k + 1], 16:, :])
+        router[:, k * 128 : (k + 1) * 128] = jnp.concatenate([low, high], axis=0)
     for s in range(S):
         spread[s] = scale
     for g in range(4):
@@ -181,7 +183,7 @@
         out_specs=[whole(), whole()],
         out_shape=[
             pltpu.VMEM((2 * E, R, C), jnp.float32),
-            pltpu.VMEM((S, 16, 128), jnp.float32),
+            pltpu.VMEM((S, 24, 128), jnp.bfloat16),
         ],
         scratch_shapes=[
             pltpu.VMEM((4, E, R, C), jnp.float32),

time: 105 us -> 105 us (level)
  no operation moved by 1% of the time
where the time goes in v2:
time: 105 us
  waiting for transfers between devices  53.2 us (51%)
  blocking collectives  23.8 us (23%)
  Pallas kernels  13.8 us (13%)
  starting transfers between devices  11.2 us (11%)
  local copies, waits for them, and re-layouts  1.97 us (2%)
    all_to_all x1, waiting for transfers between devices, exchange(): lax.all_to_all(x, 'shard', split_axis=0, concat_axis=0, tiled=True, axis_...  51.1 us
    all_to_all x2, blocking collectives, exchange(): lax.all_to_all(x, 'shard', split_axis=0, concat_axis=0, tiled=True, axis_...  23.8 us
    pallas_call x1, Pallas kernels, serve_step(): pl.pallas_call(merge_kernel, in_specs=[pl.BlockSpec(memory_space=pltpu.SM...  7.04 us
    ppermute x3, starting transfers between devices, serve_step(): lax.ppermute(router, 'expert', [(z, (z + k) % 4) for z in range(4)])  5.68 us
    all_to_all x1, starting transfers between devices, exchange(): lax.all_to_all(x, 'shard', split_axis=0, concat_axis=0, tiled=True, axis_...  5.54 us
    pallas_call x1, Pallas kernels, serve_step(): pl.pallas_call(unpack_kernel, in_specs=[whole()] * 5, out_specs=[remote()...  4.73 us
  transfers between devices with their start and end apart: 4, of which 3 were waited for; matrix products, arithmetic and copies ran while one was open for 0% of the time, Pallas kernels for 0%

profile of v2, /device:TPU:34, one launch (start us, length us, event | category | flops | bytes accessed | tf_op | source)
XLA Modules:
  0.0 104.6 jit_solution(9767776431850923355)
XLA Ops:
  0.6 7.0 %merge.1 = (f32[32,64,1024]{2,1,0:T(8,128)S(1)}, bf16[32,24,128]{2,1,0:T(8,128)(2,1)S(1)}) custom-call(f32[16]{0:T(128)} %mix.1, f32[16,64,1024]{2,1,0:T(8,128)} %a_gate.1, f32[16,64,1024]{2,1,0:T(8,128)} %b_gate.1, f32[16,64,1024]{2,1,0:T(8,128)} %a_up.1, f32[16,64,1024]{2,1,0:T(8,128)} %b_up.1, f32[16,64]{1,0:T(8,128)} %bitcast.5, f32[1,64]{1,0:T(1,128)} %bitcast.6), custom_call_target="tpu_custom_call" | custom-call | tf_op jit(solution)/shard_map/merge/pallas_call | solution.py:180
  7.7 13.3 %all_to_all.15.parts = bf16[32,24,128]{2,1,0:T(8,128)(2,1)S(1)} all-to-all(bf16[32,24,128]{2,1,0:T(8,128)(2,1)S(1)} %get-tuple-element.15), channel_id=1, replica_groups={{13,3,31,6,26,27,11,25,4,18,9,17,30,0,16,15,7,12,24,1,5,23,22,28,10,20,..., dimensions={0} | all-to-all | bytes 393216 | tf_op jit(solution)/shard_map/all_to_all | solution.py:174
  21.0 0.7 scale.1
  21.7 10.4 %all_to_all.16.scales = f32[32,8,128]{2,1,0:T(8,128)S(1)} all-to-all(f32[32,8,128]{2,1,0:T(8,128)S(1)} %get-tuple-element.16), channel_id=1, replica_groups={{13,3,31,6,26,27,11,25,4,18,9,17,30,0,16,15,7,12,24,1,5,23,22,28,10,20,..., dimensions={0} | all-to-all | bytes 262144 | tf_op jit(solution)/shard_map/all_to_all | solution.py:174
  32.2 1.3 %pack.1 = bf16[32,512,128]{2,1,0:T(8,128)(2,1)S(1)} custom-call(f32[32,64,1024]{2,1,0:T(8,128)S(1)} %get-tuple-element.14.merged, f32[32,8,128]{2,1,0:T(8,128)S(1)} %all_to_all.16.scales), custom_call_target="tpu_custom_call" | custom-call | tf_op jit(solution)/shard_map/pack/pallas_call | solution.py:225
  33.5 0.0 copy-start
  33.5 2.0 %copy-done = bf16[32,512,128]{2,1,0:T(8,128)(2,1)} copy-done((bf16[32,512,128]{2,1,0:T(8,128)(2,1)}, bf16[32,512,128]{2,1,0:T(8,128)(2,1)S(1)}, u32[]{:S(2)}) %copy-start) | copy-done | bytes 4194328
  35.4 5.5 %all-to-all-start.2 = ((bf16[32,512,128]{2,1,0:T(8,128)(2,1)}), bf16[32,512,128]{2,1,0:T(8,128)(2,1)}, u32[]{:S(2)}, u32[]{:S(2)}) async-start(bf16[32,512,128]{2,1,0:T(8,128)(2,1)} %copy-done), calls=%async_computation.2 | async-start | bytes 8388608 | tf_op jit(solution)/shard_map/all_to_all | solution.py:174
  41.0 0.2 collective-permute-start.2
  41.2 3.3 %collective-permute-start.1 = (bf16[16,2048]{1,0:T(8,128)(2,1)S(1)}, bf16[16,2048]{1,0:T(8,128)(2,1)S(1)}, u32[]{:S(2)}, u32[]{:S(2)}) collective-permute-start(bf16[16,2048]{1,0:T(8,128)(2,1)S(1)} %get-tuple-element.17.r0), channel_id=1, source_target_pairs={{0,64},{32,96},{64,0},{96,32},{1,65},{33,97},{65,1},{97,33},{2,66}... | collective-permute-start | bytes 196616 | tf_op jit(solution)/shard_map/ppermute | solution.py:220
  44.4 2.2 %collective-permute-start = (bf16[16,2048]{1,0:T(8,128)(2,1)S(1)}, bf16[16,2048]{1,0:T(8,128)(2,1)S(1)}, u32[]{:S(2)}, u32[]{:S(2)}) collective-permute-start(bf16[16,2048]{1,0:T(8,128)(2,1)S(1)} %get-tuple-element.17.r0), channel_id=1, source_target_pairs={{0,32},{32,64},{64,96},{96,0},{1,33},{33,65},{65,97},{97,1},{2,34}... | collective-permute-start | bytes 196616 | tf_op jit(solution)/shard_map/ppermute | solution.py:220
  46.7 0.0 collective-permute-done.2.r3
  46.7 1.1 %collective-permute-done.1.r2 = bf16[16,2048]{1,0:T(8,128)(2,1)S(1)} collective-permute-done((bf16[16,2048]{1,0:T(8,128)(2,1)S(1)}, bf16[16,2048]{1,0:T(8,128)(2,1)S(1)}, u32[]{:S(2)}, u32[]{:S(2)}) %collective-permute-start.1) | collective-permute-done | bytes 65568 | tf_op jit(solution)/shard_map/ppermute | solution.py:220
  47.7 1.0 collective-permute-done.r1
  48.7 51.1 %all-to-all-done.2.arrived = bf16[32,512,128]{2,1,0:T(8,128)(2,1)} async-done(((bf16[32,512,128]{2,1,0:T(8,128)(2,1)}), bf16[32,512,128]{2,1,0:T(8,128)(2,1)}, u32[]{:S(2)}, u32[]{:S(2)}) %all-to-all-start.2) | async-done | bytes 4194336 | tf_op jit(solution)/shard_map/all_to_all | solution.py:174
  99.8 4.7 %unpack.1 = (bf16[16,32,2048]{2,1,0:T(8,128)(2,1)}, bf16[16,32,2048]{2,1,0:T(8,128)(2,1)}, bf16[64,2048]{1,0:T(8,128)(2,1)}) custom-call(bf16[32,512,128]{2,1,0:T(8,128)(2,1)} %all-to-all-done.2.arrived, bf16[16,2048]{1,0:T(8,128)(2,1)S(1)} %get-tuple-element.17.r0, bf16[16,2048]{1,0:T(8,128)(2,1)S(1)} %collective-permute-done.r1, ...), custom_call_target="tpu_custom_call" | custom-call | tf_op jit(solution)/shard_map/unpack/pallas_call | solution.py:236
Async XLA Ops:
  33.5 2.0 %copy-start = (bf16[32,512,128]{2,1,0:T(8,128)(2,1)}, bf16[32,512,128]{2,1,0:T(8,128)(2,1)S(1)}, u32[]{:S(2)}) copy-start(bf16[32,512,128]{2,1,0:T(8,128)(2,1)S(1)} %pack.1) | copy-start | bytes 12582916
  35.4 64.4 %all-to-all-start.2 = ((bf16[32,512,128]{2,1,0:T(8,128)(2,1)}), bf16[32,512,128]{2,1,0:T(8,128)(2,1)}, u32[]{:S(2)}, u32[]{:S(2)}) async-start(bf16[32,512,128]{2,1,0:T(8,128)(2,1)} %copy-done), calls=%async_computation.2 | async-start | bytes 8388608 | tf_op jit(solution)/shard_map/all_to_all | solution.py:174
  41.0 5.7 %collective-permute-start.2 = (bf16[16,2048]{1,0:T(8,128)(2,1)S(1)}, bf16[16,2048]{1,0:T(8,128)(2,1)S(1)}, u32[]{:S(2)}, u32[]{:S(2)}) collective-permute-start(bf16[16,2048]{1,0:T(8,128)(2,1)S(1)} %get-tuple-element.17.r0), channel_id=1, source_target_pairs={{0,96},{32,0},{64,32},{96,64},{1,97},{33,1},{65,33},{97,65},{2,98}... | collective-permute-start | bytes 196616 | tf_op jit(solution)/shard_map/ppermute | solution.py:220
  41.2 6.6 %collective-permute-start.1 = (bf16[16,2048]{1,0:T(8,128)(2,1)S(1)}, bf16[16,2048]{1,0:T(8,128)(2,1)S(1)}, u32[]{:S(2)}, u32[]{:S(2)}) collective-permute-start(bf16[16,2048]{1,0:T(8,128)(2,1)S(1)} %get-tuple-element.17.r0), channel_id=1, source_target_pairs={{0,64},{32,96},{64,0},{96,32},{1,65},{33,97},{65,1},{97,33},{2,66}... | collective-permute-start | bytes 196616 | tf_op jit(solution)/shard_map/ppermute | solution.py:220
  44.4 4.3 %collective-permute-start = (bf16[16,2048]{1,0:T(8,128)(2,1)S(1)}, bf16[16,2048]{1,0:T(8,128)(2,1)S(1)}, u32[]{:S(2)}, u32[]{:S(2)}) collective-permute-start(bf16[16,2048]{1,0:T(8,128)(2,1)S(1)} %get-tuple-element.17.r0), channel_id=1, source_target_pairs={{0,32},{32,64},{64,96},{96,0},{1,33},{33,65},{65,97},{97,1},{2,34}... | collective-permute-start | bytes 196616 | tf_op jit(solution)/shard_map/ppermute | solution.py:220

commit v3 on v2

--- a/solution.py
+++ b/solution.py
@@ -88,7 +88,7 @@
             sums[PLACE[j * 4 + dd], 8:16, :] = rest
 
 
-def scale_kernel(parts, spread, router, scale_gate, scale_up):
+def scale_kernel(parts, spread, router):
     both = parts[:, :8, :].astype(jnp.float32) + parts[:, 8:16, :].astype(jnp.float32)
     scale = jnp.sum(both, axis=0) / D_MODEL
     for k in range(S // 2):
@@ -96,9 +96,6 @@
         router[:, k * 128 : (k + 1) * 128] = jnp.concatenate([low, high], axis=0)
     for s in range(S):
         spread[s] = scale
-    for g in range(4):
-        out = scale_gate if g < 2 else scale_up
-        out[(g % 2) * 8 : (g % 2) * 8 + 8, :] = scale[:, g * W : (g + 1) * W]
 
 
 def pack_kernel(merged, scales, packed, inverse):
@@ -122,8 +119,9 @@
 
 
 def unpack_kernel(
-    arrived, r0, r1, r2, r3, out_gate, out_up, out_router, joined, out_sems, router_sems
+    arrived, spread, r0, r1, r2, r3, out_gate, out_up, out_router, scale_gate, scale_up, *scratch
 ):
+    joined, scales, out_sems, router_sems, scale_sems = scratch
     me = lax.axis_index("expert")
     routers = (r0, r1, r2, r3)
 
@@ -150,12 +148,23 @@
 
     for k in range(4):
         serve(k).start()
+    for g in range(4):
+        rows = slice((g % 2) * 8, (g % 2) * 8 + 8)
+        scales[g // 2, rows, :] = spread[0, :, g * W : (g + 1) * W]
+    scaled = [
+        pltpu.make_async_copy(scales.at[t], out, scale_sems.at[t])
+        for t, out in enumerate((scale_gate, scale_up))
+    ]
+    for each in scaled:
+        each.start()
     lax.fori_loop(0, PAIRS, step, 0)
     for p in range(PAIRS):
         for t in range(2):
             give(t, p).wait()
     for k in range(4):
         serve(k).wait()
+    for each in scaled:
+        each.wait()
 
 
 def whole():
@@ -203,15 +212,13 @@
 
     parts = exchange(sums)
 
-    spread, router, scale_gate, scale_up = pl.pallas_call(
+    spread, router = pl.pallas_call(
         scale_kernel,
         in_specs=[whole()],
-        out_specs=[whole()] * 4,
+        out_specs=[whole()] * 2,
         out_shape=[
             pltpu.VMEM((S, 8, 128), jnp.float32),
             pltpu.VMEM((E, S * R), jnp.bfloat16),
-            jax.ShapeDtypeStruct((E, W), jnp.float32),
-            jax.ShapeDtypeStruct((E, W), jnp.float32),
         ],
         compiler_params=params(4),
         name="scale",
@@ -233,20 +240,23 @@
     )(merged, scales)
     arrived = pltpu.with_memory_space_constraint(exchange(packed), pltpu.VMEM)
 
-    final_gate, final_up, serve_router = pl.pallas_call(
+    final_gate, final_up, serve_router, scale_gate, scale_up = pl.pallas_call(
         unpack_kernel,
-        in_specs=[whole()] * 5,
-        out_specs=[remote()] * 3,
+        in_specs=[whole()] * 6,
+        out_specs=[remote()] * 5,
         out_shape=[jax.ShapeDtypeStruct((E, W, S * R), jnp.bfloat16)] * 2
-        + [jax.ShapeDtypeStruct((4 * E, S * R), jnp.bfloat16)],
+        + [jax.ShapeDtypeStruct((4 * E, S * R), jnp.bfloat16)]
+        + [jax.ShapeDtypeStruct((E, W), jnp.float32)] * 2,
         scratch_shapes=[
             pltpu.VMEM((2, E, W, S * R), jnp.bfloat16),
+            pltpu.VMEM((2, E, W), jnp.float32),
             pltpu.SemaphoreType.DMA((2, PAIRS)),
             pltpu.SemaphoreType.DMA((4,)),
+            pltpu.SemaphoreType.DMA((2,)),
         ],
         compiler_params=params(10),
         name="unpack",
-    )(arrived, router, *hops)
+    )(arrived, spread, router, *hops)
     return (
         final_gate.transpose(0, 2, 1),
         final_up.transpose(0, 2, 1),

time: 105 us -> 104 us (level)
  no operation moved by 1% of the time
where the time goes in v3:
time: 104 us
  waiting for transfers between devices  53.2 us (51%)
  blocking collectives  23.8 us (23%)
  Pallas kernels  13.2 us (13%)
  starting transfers between devices  11.2 us (11%)
  local copies, waits for them, and re-layouts  1.97 us (2%)
    all_to_all x1, waiting for transfers between devices, exchange(): lax.all_to_all(x, 'shard', split_axis=0, concat_axis=0, tiled=True, axis_...  51.1 us
    all_to_all x2, blocking collectives, exchange(): lax.all_to_all(x, 'shard', split_axis=0, concat_axis=0, tiled=True, axis_...  23.8 us
    pallas_call x1, Pallas kernels, serve_step(): pl.pallas_call(merge_kernel, in_specs=[pl.BlockSpec(memory_space=pltpu.SM...  7.04 us
    ppermute x3, starting transfers between devices, serve_step(): lax.ppermute(router, 'expert', [(z, (z + k) % 4) for z in range(4)])  5.68 us
    all_to_all x1, starting transfers between devices, exchange(): lax.all_to_all(x, 'shard', split_axis=0, concat_axis=0, tiled=True, axis_...  5.54 us
    pallas_call x1, Pallas kernels, serve_step(): pl.pallas_call(unpack_kernel, in_specs=[whole()] * 6, out_specs=[remote()...  4.82 us
  transfers between devices with their start and end apart: 4, of which 3 were waited for; matrix products, arithmetic and copies ran while one was open for 0% of the time, Pallas kernels for 0%

profile of v3, /device:TPU:34, one launch (start us, length us, event | category | flops | bytes accessed | tf_op | source)
XLA Modules:
  0.0 104.0 jit_solution(16068770404138621149)
XLA Ops:
  0.6 7.0 %merge.1 = (f32[32,64,1024]{2,1,0:T(8,128)S(1)}, bf16[32,24,128]{2,1,0:T(8,128)(2,1)S(1)}) custom-call(f32[16]{0:T(128)} %mix.1, f32[16,64,1024]{2,1,0:T(8,128)} %a_gate.1, f32[16,64,1024]{2,1,0:T(8,128)} %b_gate.1, f32[16,64,1024]{2,1,0:T(8,128)} %a_up.1, f32[16,64,1024]{2,1,0:T(8,128)} %b_up.1, f32[16,64]{1,0:T(8,128)} %bitcast.5, f32[1,64]{1,0:T(1,128)} %bitcast.6), custom_call_target="tpu_custom_call" | custom-call | tf_op jit(solution)/shard_map/merge/pallas_call | solution.py:189
  7.7 13.3 %all_to_all.15.parts = bf16[32,24,128]{2,1,0:T(8,128)(2,1)S(1)} all-to-all(bf16[32,24,128]{2,1,0:T(8,128)(2,1)S(1)} %get-tuple-element.15), channel_id=1, replica_groups={{13,3,31,6,26,27,11,25,4,18,9,17,30,0,16,15,7,12,24,1,5,23,22,28,10,20,..., dimensions={0} | all-to-all | bytes 393216 | tf_op jit(solution)/shard_map/all_to_all | solution.py:183
  21.0 0.1 scale.1
  21.1 10.5 %all_to_all.16.scales = f32[32,8,128]{2,1,0:T(8,128)S(1)} all-to-all(f32[32,8,128]{2,1,0:T(8,128)S(1)} %get-tuple-element.16.spread), channel_id=1, replica_groups={{13,3,31,6,26,27,11,25,4,18,9,17,30,0,16,15,7,12,24,1,5,23,22,28,10,20,..., dimensions={0} | all-to-all | bytes 262144 | tf_op jit(solution)/shard_map/all_to_all | solution.py:183
  31.6 1.3 %pack.1 = bf16[32,512,128]{2,1,0:T(8,128)(2,1)S(1)} custom-call(f32[32,64,1024]{2,1,0:T(8,128)S(1)} %get-tuple-element.14.merged, f32[32,8,128]{2,1,0:T(8,128)S(1)} %all_to_all.16.scales), custom_call_target="tpu_custom_call" | custom-call | tf_op jit(solution)/shard_map/pack/pallas_call | solution.py:232
  32.9 0.0 copy-start
  32.9 2.0 %copy-done = bf16[32,512,128]{2,1,0:T(8,128)(2,1)} copy-done((bf16[32,512,128]{2,1,0:T(8,128)(2,1)}, bf16[32,512,128]{2,1,0:T(8,128)(2,1)S(1)}, u32[]{:S(2)}) %copy-start) | copy-done | bytes 4194328
  34.8 5.5 %all-to-all-start.2 = ((bf16[32,512,128]{2,1,0:T(8,128)(2,1)}), bf16[32,512,128]{2,1,0:T(8,128)(2,1)}, u32[]{:S(2)}, u32[]{:S(2)}) async-start(bf16[32,512,128]{2,1,0:T(8,128)(2,1)} %copy-done), calls=%async_computation.2 | async-start | bytes 8388608 | tf_op jit(solution)/shard_map/all_to_all | solution.py:183
  40.4 0.2 collective-permute-start.2
  40.6 3.3 %collective-permute-start.1 = (bf16[16,2048]{1,0:T(8,128)(2,1)S(1)}, bf16[16,2048]{1,0:T(8,128)(2,1)S(1)}, u32[]{:S(2)}, u32[]{:S(2)}) collective-permute-start(bf16[16,2048]{1,0:T(8,128)(2,1)S(1)} %get-tuple-element.17.r0), channel_id=1, source_target_pairs={{0,64},{32,96},{64,0},{96,32},{1,65},{33,97},{65,1},{97,33},{2,66}... | collective-permute-start | bytes 196616 | tf_op jit(solution)/shard_map/ppermute | solution.py:227
  43.8 2.2 %collective-permute-start = (bf16[16,2048]{1,0:T(8,128)(2,1)S(1)}, bf16[16,2048]{1,0:T(8,128)(2,1)S(1)}, u32[]{:S(2)}, u32[]{:S(2)}) collective-permute-start(bf16[16,2048]{1,0:T(8,128)(2,1)S(1)} %get-tuple-element.17.r0), channel_id=1, source_target_pairs={{0,32},{32,64},{64,96},{96,0},{1,33},{33,65},{65,97},{97,1},{2,34}... | collective-permute-start | bytes 196616 | tf_op jit(solution)/shard_map/ppermute | solution.py:227
  46.1 0.0 collective-permute-done.2.r3
  46.1 1.1 %collective-permute-done.1.r2 = bf16[16,2048]{1,0:T(8,128)(2,1)S(1)} collective-permute-done((bf16[16,2048]{1,0:T(8,128)(2,1)S(1)}, bf16[16,2048]{1,0:T(8,128)(2,1)S(1)}, u32[]{:S(2)}, u32[]{:S(2)}) %collective-permute-start.1) | collective-permute-done | bytes 65568 | tf_op jit(solution)/shard_map/ppermute | solution.py:227
  47.1 1.0 collective-permute-done.r1
  48.1 51.1 %all-to-all-done.2.arrived = bf16[32,512,128]{2,1,0:T(8,128)(2,1)} async-done(((bf16[32,512,128]{2,1,0:T(8,128)(2,1)}), bf16[32,512,128]{2,1,0:T(8,128)(2,1)}, u32[]{:S(2)}, u32[]{:S(2)}) %all-to-all-start.2) | async-done | bytes 4194336 | tf_op jit(solution)/shard_map/all_to_all | solution.py:183
  99.2 4.8 %unpack.1 = (bf16[16,32,2048]{2,1,0:T(8,128)(2,1)}, bf16[16,32,2048]{2,1,0:T(8,128)(2,1)}, bf16[64,2048]{1,0:T(8,128)(2,1)}, f32[16,32]{1,0:T(8,128)}, f32[16,32]{1,0:T(8,128)}) custom-call(bf16[32,512,128]{2,1,0:T(8,128)(2,1)} %all-to-all-done.2.arrived, f32[32,8,128]{2,1,0:T(8,128)S(1)} %get-tuple-element.16.spread, ...), custom_call_target="tpu_custom_call" | custom-call | tf_op jit(solution)/shard_map/unpack/pallas_call | solution.py:243
Async XLA Ops:
  32.9 2.0 %copy-start = (bf16[32,512,128]{2,1,0:T(8,128)(2,1)}, bf16[32,512,128]{2,1,0:T(8,128)(2,1)S(1)}, u32[]{:S(2)}) copy-start(bf16[32,512,128]{2,1,0:T(8,128)(2,1)S(1)} %pack.1) | copy-start | bytes 12582916
  34.8 64.4 %all-to-all-start.2 = ((bf16[32,512,128]{2,1,0:T(8,128)(2,1)}), bf16[32,512,128]{2,1,0:T(8,128)(2,1)}, u32[]{:S(2)}, u32[]{:S(2)}) async-start(bf16[32,512,128]{2,1,0:T(8,128)(2,1)} %copy-done), calls=%async_computation.2 | async-start | bytes 8388608 | tf_op jit(solution)/shard_map/all_to_all | solution.py:183
  40.4 5.7 %collective-permute-start.2 = (bf16[16,2048]{1,0:T(8,128)(2,1)S(1)}, bf16[16,2048]{1,0:T(8,128)(2,1)S(1)}, u32[]{:S(2)}, u32[]{:S(2)}) collective-permute-start(bf16[16,2048]{1,0:T(8,128)(2,1)S(1)} %get-tuple-element.17.r0), channel_id=1, source_target_pairs={{0,96},{32,0},{64,32},{96,64},{1,97},{33,1},{65,33},{97,65},{2,98}... | collective-permute-start | bytes 196616 | tf_op jit(solution)/shard_map/ppermute | solution.py:227
  40.6 6.6 %collective-permute-start.1 = (bf16[16,2048]{1,0:T(8,128)(2,1)S(1)}, bf16[16,2048]{1,0:T(8,128)(2,1)S(1)}, u32[]{:S(2)}, u32[]{:S(2)}) collective-permute-start(bf16[16,2048]{1,0:T(8,128)(2,1)S(1)} %get-tuple-element.17.r0), channel_id=1, source_target_pairs={{0,64},{32,96},{64,0},{96,32},{1,65},{33,97},{65,1},{97,33},{2,66}... | collective-permute-start | bytes 196616 | tf_op jit(solution)/shard_map/ppermute | solution.py:227
  43.8 4.3 %collective-permute-start = (bf16[16,2048]{1,0:T(8,128)(2,1)S(1)}, bf16[16,2048]{1,0:T(8,128)(2,1)S(1)}, u32[]{:S(2)}, u32[]{:S(2)}) collective-permute-start(bf16[16,2048]{1,0:T(8,128)(2,1)S(1)} %get-tuple-element.17.r0), channel_id=1, source_target_pairs={{0,32},{32,64},{64,96},{96,0},{1,33},{33,65},{65,97},{97,1},{2,34}... | collective-permute-start | bytes 196616 | tf_op jit(solution)/shard_map/ppermute | solution.py:227

commit v4 on v3

--- a/solution.py
+++ b/solution.py
@@ -41,22 +41,26 @@
 
 
 def merge_kernel(
-    mix, a_gate, b_gate, a_up, b_up, router, gain, merged, sums, inputs, row_sums, sems
+    shares, a_gate, b_gate, a_up, b_up, weight, gains, merged, sums, *scratch
 ):
+    inputs, row_sums, mix, router, gain, sems, small_sems = scratch
+
     def copy(k, source, pair):
         return pltpu.make_async_copy(
             source.at[pl.ds(2 * pair, 2)], inputs.at[k, pl.ds(2 * pair, 2)], sems.at[k, pair]
         )
 
+    small = [
+        pltpu.make_async_copy(source, target, small_sems.at[k])
+        for k, (source, target) in enumerate(((shares, mix), (weight, router), (gains, gain)))
+    ]
+    for each in small:
+        each.start()
     sources = (a_gate, b_gate, a_up, b_up)
     for pair in range(PAIRS):
         for k, source in enumerate(sources):
             copy(k, source, pair).start()
-
-    served = router[...] * gain[...]
-    served = jnp.concatenate([served[:8], served[8:]], axis=1).astype(jnp.bfloat16)
-    for s in range(S):
-        sums[s, 16:, :] = served
+    small[0].wait()
     sublane = lax.broadcasted_iota(jnp.int32, (8, 128), 0)
 
     def step(pair, carry):
@@ -79,6 +83,13 @@
         return carry
 
     lax.fori_loop(0, PAIRS, step, 0)
+    for each in small[1:]:
+        each.wait()
+
+    served = router[...] * gain[...]
+    served = jnp.concatenate([served[:8], served[8:]], axis=1).astype(jnp.bfloat16)
+    for s in range(S):
+        sums[s, 16:, :] = served
     for j in range(C // 128):
         tiles = regroup([row_sums[g, :, j * 128 : (j + 1) * 128] for g in range(4)])
         for dd in range(4):
@@ -188,7 +199,7 @@
 def serve_step(master_gate, second_gate, master_up, second_up, mix_share, router_weight, router_gain):
     merged, sums = pl.pallas_call(
         merge_kernel,
-        in_specs=[pl.BlockSpec(memory_space=pltpu.SMEM)] + [remote()] * 4 + [whole()] * 2,
+        in_specs=[remote()] * 7,
         out_specs=[whole(), whole()],
         out_shape=[
             pltpu.VMEM((2 * E, R, C), jnp.float32),
@@ -197,7 +208,11 @@
         scratch_shapes=[
             pltpu.VMEM((4, E, R, C), jnp.float32),
             pltpu.VMEM((4, 8, C), jnp.float32),
+            pltpu.SMEM((E,), jnp.float32),
+            pltpu.VMEM((E, R), jnp.float32),
+            pltpu.VMEM((1, R), jnp.float32),
             pltpu.SemaphoreType.DMA((4, PAIRS)),
+            pltpu.SemaphoreType.DMA((3,)),
         ],
         compiler_params=params(20),
         name="merge",

time: 104 us -> 104 us (level)
  the two profiles are of different devices: /device:TPU:34 before, /device:TPU:2 now
where the time goes in v4:
time: 104 us; the launch traced here: 103 us
  waiting for transfers between devices  53.5 us (51%)
  blocking collectives  23.8 us (23%)
  Pallas kernels  12.6 us (12%)
  starting transfers between devices  10.9 us (10%)
  local copies, waits for them, and re-layouts  1.97 us (2%)
    all_to_all x1, waiting for transfers between devices, exchange(): lax.all_to_all(x, 'shard', split_axis=0, concat_axis=0, tiled=True, axis_...  48.5 us
    all_to_all x2, blocking collectives, exchange(): lax.all_to_all(x, 'shard', split_axis=0, concat_axis=0, tiled=True, axis_...  23.8 us
    pallas_call x1, Pallas kernels, serve_step(): pl.pallas_call(merge_kernel, in_specs=[remote()] * 7, out_specs=[whole(),...  6.38 us
    all_to_all x1, starting transfers between devices, exchange(): lax.all_to_all(x, 'shard', split_axis=0, concat_axis=0, tiled=True, axis_...  5.54 us
    ppermute x3, starting transfers between devices, serve_step(): lax.ppermute(router, 'expert', [(z, (z + k) % 4) for z in range(4)])  5.37 us
    ppermute x3, waiting for transfers between devices, serve_step(): lax.ppermute(router, 'expert', [(z, (z + k) % 4) for z in range(4)])  5 us
    pallas_call x1, Pallas kernels, serve_step(): pl.pallas_call(unpack_kernel, in_specs=[whole()] * 6, out_specs=[remote()...  4.82 us
  transfers between devices with their start and end apart: 4, of which 4 were waited for; matrix products, arithmetic and copies ran while one was open for 0% of the time, Pallas kernels for 0%

profile of v4, /device:TPU:2, one launch (start us, length us, event | category | flops | bytes accessed | tf_op | source)
XLA Modules:
  0.0 103.4 jit_solution(10243974905577659363)
XLA Ops:
  0.6 6.4 %merge.1 = (f32[32,64,1024]{2,1,0:T(8,128)S(1)}, bf16[32,24,128]{2,1,0:T(8,128)(2,1)S(1)}) custom-call(f32[16]{0:T(128)} %shares.1, f32[16,64,1024]{2,1,0:T(8,128)} %a_gate.1, f32[16,64,1024]{2,1,0:T(8,128)} %b_gate.1, f32[16,64,1024]{2,1,0:T(8,128)} %a_up.1, f32[16,64,1024]{2,1,0:T(8,128)} %b_up.1, f32[16,64]{1,0:T(8,128)} %bitcast.5, f32[1,64]{1,0:T(1,128)} %bitcast.6), custom_call_target="tpu_custom_call" | custom-call | tf_op jit(solution)/shard_map/merge/pallas_call | solution.py:200
  7.0 13.3 %all_to_all.15.parts = bf16[32,24,128]{2,1,0:T(8,128)(2,1)S(1)} all-to-all(bf16[32,24,128]{2,1,0:T(8,128)(2,1)S(1)} %get-tuple-element.15), channel_id=1, replica_groups={{13,3,31,6,26,27,11,25,4,18,9,17,30,0,16,15,7,12,24,1,5,23,22,28,10,20,..., dimensions={0} | all-to-all | bytes 393216 | tf_op jit(solution)/shard_map/all_to_all | solution.py:194
  20.4 0.1 scale.1
  20.5 10.5 %all_to_all.16.scales = f32[32,8,128]{2,1,0:T(8,128)S(1)} all-to-all(f32[32,8,128]{2,1,0:T(8,128)S(1)} %get-tuple-element.16.spread), channel_id=1, replica_groups={{13,3,31,6,26,27,11,25,4,18,9,17,30,0,16,15,7,12,24,1,5,23,22,28,10,20,..., dimensions={0} | all-to-all | bytes 262144 | tf_op jit(solution)/shard_map/all_to_all | solution.py:194
  30.9 1.3 %pack.1 = bf16[32,512,128]{2,1,0:T(8,128)(2,1)S(1)} custom-call(f32[32,64,1024]{2,1,0:T(8,128)S(1)} %get-tuple-element.14.merged, f32[32,8,128]{2,1,0:T(8,128)S(1)} %all_to_all.16.scales), custom_call_target="tpu_custom_call" | custom-call | tf_op jit(solution)/shard_map/pack/pallas_call | solution.py:247
  32.2 0.0 copy-start
  32.2 2.0 %copy-done = bf16[32,512,128]{2,1,0:T(8,128)(2,1)} copy-done((bf16[32,512,128]{2,1,0:T(8,128)(2,1)}, bf16[32,512,128]{2,1,0:T(8,128)(2,1)S(1)}, u32[]{:S(2)}) %copy-start) | copy-done | bytes 4194328
  34.2 5.5 %all-to-all-start.2 = ((bf16[32,512,128]{2,1,0:T(8,128)(2,1)}), bf16[32,512,128]{2,1,0:T(8,128)(2,1)}, u32[]{:S(2)}, u32[]{:S(2)}) async-start(bf16[32,512,128]{2,1,0:T(8,128)(2,1)} %copy-done), calls=%async_computation.2 | async-start | bytes 8388608 | tf_op jit(solution)/shard_map/all_to_all | solution.py:194
  39.7 4.1 %collective-permute-start.2 = (bf16[16,2048]{1,0:T(8,128)(2,1)S(1)}, bf16[16,2048]{1,0:T(8,128)(2,1)S(1)}, u32[]{:S(2)}, u32[]{:S(2)}) collective-permute-start(bf16[16,2048]{1,0:T(8,128)(2,1)S(1)} %get-tuple-element.17.r0), channel_id=1, source_target_pairs={{0,96},{32,0},{64,32},{96,64},{1,97},{33,1},{65,33},{97,65},{2,98}... | collective-permute-start | bytes 196616 | tf_op jit(solution)/shard_map/ppermute | solution.py:242
  43.8 0.0 collective-permute-start.1
  43.8 1.3 %collective-permute-start = (bf16[16,2048]{1,0:T(8,128)(2,1)S(1)}, bf16[16,2048]{1,0:T(8,128)(2,1)S(1)}, u32[]{:S(2)}, u32[]{:S(2)}) collective-permute-start(bf16[16,2048]{1,0:T(8,128)(2,1)S(1)} %get-tuple-element.17.r0), channel_id=1, source_target_pairs={{0,32},{32,64},{64,96},{96,0},{1,33},{33,65},{65,97},{97,1},{2,34}... | collective-permute-start | bytes 196616 | tf_op jit(solution)/shard_map/ppermute | solution.py:242
  45.1 1.6 %collective-permute-done.2.r3 = bf16[16,2048]{1,0:T(8,128)(2,1)S(1)} collective-permute-done((bf16[16,2048]{1,0:T(8,128)(2,1)S(1)}, bf16[16,2048]{1,0:T(8,128)(2,1)S(1)}, u32[]{:S(2)}, u32[]{:S(2)}) %collective-permute-start.2) | collective-permute-done | bytes 65568 | tf_op jit(solution)/shard_map/ppermute | solution.py:242
  46.7 3.0 %collective-permute-done.1.r2 = bf16[16,2048]{1,0:T(8,128)(2,1)S(1)} collective-permute-done((bf16[16,2048]{1,0:T(8,128)(2,1)S(1)}, bf16[16,2048]{1,0:T(8,128)(2,1)S(1)}, u32[]{:S(2)}, u32[]{:S(2)}) %collective-permute-start.1) | collective-permute-done | bytes 65568 | tf_op jit(solution)/shard_map/ppermute | solution.py:242
  49.7 0.4 collective-permute-done.r1
  50.1 48.5 %all-to-all-done.2.arrived = bf16[32,512,128]{2,1,0:T(8,128)(2,1)} async-done(((bf16[32,512,128]{2,1,0:T(8,128)(2,1)}), bf16[32,512,128]{2,1,0:T(8,128)(2,1)}, u32[]{:S(2)}, u32[]{:S(2)}) %all-to-all-start.2) | async-done | bytes 4194336 | tf_op jit(solution)/shard_map/all_to_all | solution.py:194
  98.6 4.8 %unpack.1 = (bf16[16,32,2048]{2,1,0:T(8,128)(2,1)}, bf16[16,32,2048]{2,1,0:T(8,128)(2,1)}, bf16[64,2048]{1,0:T(8,128)(2,1)}, f32[16,32]{1,0:T(8,128)}, f32[16,32]{1,0:T(8,128)}) custom-call(bf16[32,512,128]{2,1,0:T(8,128)(2,1)} %all-to-all-done.2.arrived, f32[32,8,128]{2,1,0:T(8,128)S(1)} %get-tuple-element.16.spread, ...), custom_call_target="tpu_custom_call" | custom-call | tf_op jit(solution)/shard_map/unpack/pallas_call | solution.py:258
Async XLA Ops:
  32.2 2.0 %copy-start = (bf16[32,512,128]{2,1,0:T(8,128)(2,1)}, bf16[32,512,128]{2,1,0:T(8,128)(2,1)S(1)}, u32[]{:S(2)}) copy-start(bf16[32,512,128]{2,1,0:T(8,128)(2,1)S(1)} %pack.1) | copy-start | bytes 12582916
  34.2 64.4 %all-to-all-start.2 = ((bf16[32,512,128]{2,1,0:T(8,128)(2,1)}), bf16[32,512,128]{2,1,0:T(8,128)(2,1)}, u32[]{:S(2)}, u32[]{:S(2)}) async-start(bf16[32,512,128]{2,1,0:T(8,128)(2,1)} %copy-done), calls=%async_computation.2 | async-start | bytes 8388608 | tf_op jit(solution)/shard_map/all_to_all | solution.py:194
  39.7 7.0 %collective-permute-start.2 = (bf16[16,2048]{1,0:T(8,128)(2,1)S(1)}, bf16[16,2048]{1,0:T(8,128)(2,1)S(1)}, u32[]{:S(2)}, u32[]{:S(2)}) collective-permute-start(bf16[16,2048]{1,0:T(8,128)(2,1)S(1)} %get-tuple-element.17.r0), channel_id=1, source_target_pairs={{0,96},{32,0},{64,32},{96,64},{1,97},{33,1},{65,33},{97,65},{2,98}... | collective-permute-start | bytes 196616 | tf_op jit(solution)/shard_map/ppermute | solution.py:242
  43.8 5.9 %collective-permute-start.1 = (bf16[16,2048]{1,0:T(8,128)(2,1)S(1)}, bf16[16,2048]{1,0:T(8,128)(2,1)S(1)}, u32[]{:S(2)}, u32[]{:S(2)}) collective-permute-start(bf16[16,2048]{1,0:T(8,128)(2,1)S(1)} %get-tuple-element.17.r0), channel_id=1, source_target_pairs={{0,64},{32,96},{64,0},{96,32},{1,65},{33,97},{65,1},{97,33},{2,66}... | collective-permute-start | bytes 196616 | tf_op jit(solution)/shard_map/ppermute | solution.py:242
  43.8 6.3 %collective-permute-start = (bf16[16,2048]{1,0:T(8,128)(2,1)S(1)}, bf16[16,2048]{1,0:T(8,128)(2,1)S(1)}, u32[]{:S(2)}, u32[]{:S(2)}) collective-permute-start(bf16[16,2048]{1,0:T(8,128)(2,1)S(1)} %get-tuple-element.17.r0), channel_id=1, source_target_pairs={{0,32},{32,64},{64,96},{96,0},{1,33},{33,65},{65,97},{97,1},{2,34}... | collective-permute-start | bytes 196616 | tf_op jit(solution)/shard_map/ppermute | solution.py:242

commit v5 on v4

--- a/solution.py
+++ b/solution.py
@@ -137,7 +137,7 @@
     routers = (r0, r1, r2, r3)
 
     def serve(k):
-        rows = pl.ds(pl.multiple_of(lax.rem(me + 4 - k, 4) * E, E), E)
+        rows = pl.ds(pl.multiple_of(lax.bitwise_xor(me, (0, 3, 2, 1)[k]) * E, E), E)
         return pltpu.make_async_copy(routers[k], out_router.at[rows], router_sems.at[k])
 
     def give(t, p):
@@ -148,7 +148,7 @@
 
     def step(p, carry):
         for t in range(2):
-            rows = pl.ds(pl.multiple_of((t * PAIRS + p) * W, W), W)
+            rows = slice((t * PAIRS + p) * W, (t * PAIRS + p + 1) * W)
             for k in range(S // 2):
                 cols = slice(k * 128, (k + 1) * 128)
                 even, odd = join(arrived[PLACE[2 * k], rows], arrived[PLACE[2 * k + 1], rows])
@@ -168,7 +168,8 @@
     ]
     for each in scaled:
         each.start()
-    lax.fori_loop(0, PAIRS, step, 0)
+    for p in range(PAIRS):
+        step(p, 0)
     for p in range(PAIRS):
         for t in range(2):
             give(t, p).wait()
@@ -239,8 +240,8 @@
         name="scale",
     )(parts)
     hops = [
-        lax.ppermute(router, "expert", [(z, (z + k) % 4) for z in range(4)])
-        for k in range(1, 4)
+        lax.ppermute(router, "expert", [(z, z ^ k) for z in range(4)])
+        for k in (3, 2, 1)
     ]
     scales = exchange(spread)
 

time: 104 us -> 103 us (level)
  transfers between devices with their start and end apart: 4 -> 4, of which waited for: 4 -> 3; matrix products, arithmetic and copies ran while one was open for 0% -> 0% of each run, Pallas kernels for 0% -> 0%
where the time goes in v5:
time: 103 us
  waiting for transfers between devices  53.3 us (52%)
  blocking collectives  23.8 us (23%)
  Pallas kernels  12.4 us (12%)
  starting transfers between devices  11.1 us (11%)
  local copies, waits for them, and re-layouts  1.97 us (2%)
    all_to_all x1, waiting for transfers between devices, exchange(): lax.all_to_all(x, 'shard', split_axis=0, concat_axis=0, tiled=True, axis_...  47.8 us
    all_to_all x2, blocking collectives, exchange(): lax.all_to_all(x, 'shard', split_axis=0, concat_axis=0, tiled=True, axis_...  23.8 us
    pallas_call x1, Pallas kernels, serve_step(): pl.pallas_call(merge_kernel, in_specs=[remote()] * 7, out_specs=[whole(),...  6.38 us
    ppermute x3, starting transfers between devices, serve_step(): lax.ppermute(router, 'expert', [(z, z ^ k) for z in range(4)])  5.58 us
    all_to_all x1, starting transfers between devices, exchange(): lax.all_to_all(x, 'shard', split_axis=0, concat_axis=0, tiled=True, axis_...  5.54 us
    ppermute x3, waiting for transfers between devices, serve_step(): lax.ppermute(router, 'expert', [(z, z ^ k) for z in range(4)])  5.47 us
    pallas_call x1, Pallas kernels, serve_step(): pl.pallas_call(unpack_kernel, in_specs=[whole()] * 6, out_specs=[remote()...  4.61 us
  transfers between devices with their start and end apart: 4, of which 3 were waited for; matrix products, arithmetic and copies ran while one was open for 0% of the time, Pallas kernels for 0%

profile of v5, /device:TPU:2, one launch (start us, length us, event | category | flops | bytes accessed | tf_op | source)
XLA Modules:
  0.0 103.2 jit_solution(3730727032557327675)
XLA Ops:
  0.6 6.4 %merge.1 = (f32[32,64,1024]{2,1,0:T(8,128)S(1)}, bf16[32,24,128]{2,1,0:T(8,128)(2,1)S(1)}) custom-call(f32[16]{0:T(128)} %shares.1, f32[16,64,1024]{2,1,0:T(8,128)} %a_gate.1, f32[16,64,1024]{2,1,0:T(8,128)} %b_gate.1, f32[16,64,1024]{2,1,0:T(8,128)} %a_up.1, f32[16,64,1024]{2,1,0:T(8,128)} %b_up.1, f32[16,64]{1,0:T(8,128)} %bitcast.5, f32[1,64]{1,0:T(1,128)} %bitcast.6), custom_call_target="tpu_custom_call" | custom-call | tf_op jit(solution)/shard_map/merge/pallas_call | solution.py:201
  7.0 13.3 %all_to_all.15.parts = bf16[32,24,128]{2,1,0:T(8,128)(2,1)S(1)} all-to-all(bf16[32,24,128]{2,1,0:T(8,128)(2,1)S(1)} %get-tuple-element.15), channel_id=1, replica_groups={{13,3,31,6,26,27,11,25,4,18,9,17,30,0,16,15,7,12,24,1,5,23,22,28,10,20,..., dimensions={0} | all-to-all | bytes 393216 | tf_op jit(solution)/shard_map/all_to_all | solution.py:195
  20.4 0.1 scale.1
  20.5 10.5 %all_to_all.16.scales = f32[32,8,128]{2,1,0:T(8,128)S(1)} all-to-all(f32[32,8,128]{2,1,0:T(8,128)S(1)} %get-tuple-element.16.spread), channel_id=1, replica_groups={{13,3,31,6,26,27,11,25,4,18,9,17,30,0,16,15,7,12,24,1,5,23,22,28,10,20,..., dimensions={0} | all-to-all | bytes 262144 | tf_op jit(solution)/shard_map/all_to_all | solution.py:195
  30.9 1.3 %pack.1 = bf16[32,512,128]{2,1,0:T(8,128)(2,1)S(1)} custom-call(f32[32,64,1024]{2,1,0:T(8,128)S(1)} %get-tuple-element.14.merged, f32[32,8,128]{2,1,0:T(8,128)S(1)} %all_to_all.16.scales), custom_call_target="tpu_custom_call" | custom-call | tf_op jit(solution)/shard_map/pack/pallas_call | solution.py:248
  32.2 0.0 copy-start
  32.2 2.0 %copy-done = bf16[32,512,128]{2,1,0:T(8,128)(2,1)} copy-done((bf16[32,512,128]{2,1,0:T(8,128)(2,1)}, bf16[32,512,128]{2,1,0:T(8,128)(2,1)S(1)}, u32[]{:S(2)}) %copy-start) | copy-done | bytes 4194328
  34.2 5.5 %all-to-all-start.2 = ((bf16[32,512,128]{2,1,0:T(8,128)(2,1)}), bf16[32,512,128]{2,1,0:T(8,128)(2,1)}, u32[]{:S(2)}, u32[]{:S(2)}) async-start(bf16[32,512,128]{2,1,0:T(8,128)(2,1)} %copy-done), calls=%async_computation.2 | async-start | bytes 8388608 | tf_op jit(solution)/shard_map/all_to_all | solution.py:195
  39.7 2.0 %collective-permute-start.2 = (bf16[16,2048]{1,0:T(8,128)(2,1)S(1)}, bf16[16,2048]{1,0:T(8,128)(2,1)S(1)}, u32[]{:S(2)}, u32[]{:S(2)}) collective-permute-start(bf16[16,2048]{1,0:T(8,128)(2,1)S(1)} %get-tuple-element.17.r0), channel_id=1, source_target_pairs={{0,32},{32,0},{64,96},{96,64},{1,33},{33,1},{65,97},{97,65},{2,34}... | collective-permute-start | bytes 196616 | tf_op jit(solution)/shard_map/ppermute | solution.py:243
  41.7 3.6 %collective-permute-start.1 = (bf16[16,2048]{1,0:T(8,128)(2,1)S(1)}, bf16[16,2048]{1,0:T(8,128)(2,1)S(1)}, u32[]{:S(2)}, u32[]{:S(2)}) collective-permute-start(bf16[16,2048]{1,0:T(8,128)(2,1)S(1)} %get-tuple-element.17.r0), channel_id=1, source_target_pairs={{0,64},{32,96},{64,0},{96,32},{1,65},{33,97},{65,1},{97,33},{2,66}... | collective-permute-start | bytes 196616 | tf_op jit(solution)/shard_map/ppermute | solution.py:243
  45.3 0.0 collective-permute-start
  45.3 0.0 collective-permute-done.2.r3
  45.3 3.3 %collective-permute-done.1.r2 = bf16[16,2048]{1,0:T(8,128)(2,1)S(1)} collective-permute-done((bf16[16,2048]{1,0:T(8,128)(2,1)S(1)}, bf16[16,2048]{1,0:T(8,128)(2,1)S(1)}, u32[]{:S(2)}, u32[]{:S(2)}) %collective-permute-start.1) | collective-permute-done | bytes 65568 | tf_op jit(solution)/shard_map/ppermute | solution.py:243
  48.6 2.2 %collective-permute-done.r1 = bf16[16,2048]{1,0:T(8,128)(2,1)S(1)} collective-permute-done((bf16[16,2048]{1,0:T(8,128)(2,1)S(1)}, bf16[16,2048]{1,0:T(8,128)(2,1)S(1)}, u32[]{:S(2)}, u32[]{:S(2)}) %collective-permute-start) | collective-permute-done | bytes 65568 | tf_op jit(solution)/shard_map/ppermute | solution.py:243
  50.8 47.8 %all-to-all-done.2.arrived = bf16[32,512,128]{2,1,0:T(8,128)(2,1)} async-done(((bf16[32,512,128]{2,1,0:T(8,128)(2,1)}), bf16[32,512,128]{2,1,0:T(8,128)(2,1)}, u32[]{:S(2)}, u32[]{:S(2)}) %all-to-all-start.2) | async-done | bytes 4194336 | tf_op jit(solution)/shard_map/all_to_all | solution.py:195
  98.6 4.6 %unpack.1 = (bf16[16,32,2048]{2,1,0:T(8,128)(2,1)}, bf16[16,32,2048]{2,1,0:T(8,128)(2,1)}, bf16[64,2048]{1,0:T(8,128)(2,1)}, f32[16,32]{1,0:T(8,128)}, f32[16,32]{1,0:T(8,128)}) custom-call(bf16[32,512,128]{2,1,0:T(8,128)(2,1)} %all-to-all-done.2.arrived, f32[32,8,128]{2,1,0:T(8,128)S(1)} %get-tuple-element.16.spread, ...), custom_call_target="tpu_custom_call" | custom-call | tf_op jit(solution)/shard_map/unpack/pallas_call | solution.py:259
Async XLA Ops:
  32.2 2.0 %copy-start = (bf16[32,512,128]{2,1,0:T(8,128)(2,1)}, bf16[32,512,128]{2,1,0:T(8,128)(2,1)S(1)}, u32[]{:S(2)}) copy-start(bf16[32,512,128]{2,1,0:T(8,128)(2,1)S(1)} %pack.1) | copy-start | bytes 12582916
  34.2 64.4 %all-to-all-start.2 = ((bf16[32,512,128]{2,1,0:T(8,128)(2,1)}), bf16[32,512,128]{2,1,0:T(8,128)(2,1)}, u32[]{:S(2)}, u32[]{:S(2)}) async-start(bf16[32,512,128]{2,1,0:T(8,128)(2,1)} %copy-done), calls=%async_computation.2 | async-start | bytes 8388608 | tf_op jit(solution)/shard_map/all_to_all | solution.py:195
  39.7 5.6 %collective-permute-start.2 = (bf16[16,2048]{1,0:T(8,128)(2,1)S(1)}, bf16[16,2048]{1,0:T(8,128)(2,1)S(1)}, u32[]{:S(2)}, u32[]{:S(2)}) collective-permute-start(bf16[16,2048]{1,0:T(8,128)(2,1)S(1)} %get-tuple-element.17.r0), channel_id=1, source_target_pairs={{0,32},{32,0},{64,96},{96,64},{1,33},{33,1},{65,97},{97,65},{2,34}... | collective-permute-start | bytes 196616 | tf_op jit(solution)/shard_map/ppermute | solution.py:243
  41.7 6.9 %collective-permute-start.1 = (bf16[16,2048]{1,0:T(8,128)(2,1)S(1)}, bf16[16,2048]{1,0:T(8,128)(2,1)S(1)}, u32[]{:S(2)}, u32[]{:S(2)}) collective-permute-start(bf16[16,2048]{1,0:T(8,128)(2,1)S(1)} %get-tuple-element.17.r0), channel_id=1, source_target_pairs={{0,64},{32,96},{64,0},{96,32},{1,65},{33,97},{65,1},{97,33},{2,66}... | collective-permute-start | bytes 196616 | tf_op jit(solution)/shard_map/ppermute | solution.py:243
  45.3 5.5 %collective-permute-start = (bf16[16,2048]{1,0:T(8,128)(2,1)S(1)}, bf16[16,2048]{1,0:T(8,128)(2,1)S(1)}, u32[]{:S(2)}, u32[]{:S(2)}) collective-permute-start(bf16[16,2048]{1,0:T(8,128)(2,1)S(1)} %get-tuple-element.17.r0), channel_id=1, source_target_pairs={{0,96},{32,64},{64,32},{96,0},{1,97},{33,65},{65,33},{97,1},{2,98}... | collective-permute-start | bytes 196616 | tf_op jit(solution)/shard_map/ppermute | solution.py:243

commit v6 on v5

--- a/solution.py
+++ b/solution.py
@@ -137,7 +137,7 @@
     routers = (r0, r1, r2, r3)
 
     def serve(k):
-        rows = pl.ds(pl.multiple_of(lax.bitwise_xor(me, (0, 3, 2, 1)[k]) * E, E), E)
+        rows = pl.ds(pl.multiple_of(lax.bitwise_xor(me, k) * E, E), E)
         return pltpu.make_async_copy(routers[k], out_router.at[rows], router_sems.at[k])
 
     def give(t, p):
@@ -157,6 +157,8 @@
             give(t, p).start()
         return carry
 
+    for p in range(2):
+        step(p, 0)
     for k in range(4):
         serve(k).start()
     for g in range(4):
@@ -168,7 +170,7 @@
     ]
     for each in scaled:
         each.start()
-    for p in range(PAIRS):
+    for p in range(2, PAIRS):
         step(p, 0)
     for p in range(PAIRS):
         for t in range(2):
@@ -241,7 +243,7 @@
     )(parts)
     hops = [
         lax.ppermute(router, "expert", [(z, z ^ k) for z in range(4)])
-        for k in (3, 2, 1)
+        for k in range(1, 4)
     ]
     scales = exchange(spread)
 

time: 103 us -> 103 us (level)
    all_to_all x1, waiting for transfers between devices: 47.8 us -> 48.9 us  [exchange(): lax.all_to_all(x, 'shard', split_axis=0, concat_axis=0, tiled=True, axis_...]
where the time goes in v6:
time: 103 us
  waiting for transfers between devices  53.8 us (52%)
  blocking collectives  23.8 us (23%)
  Pallas kernels  12.4 us (12%)
  starting transfers between devices  10.6 us (10%)
  local copies, waits for them, and re-layouts  1.97 us (2%)
    all_to_all x1, waiting for transfers between devices, exchange(): lax.all_to_all(x, 'shard', split_axis=0, concat_axis=0, tiled=True, axis_...  48.9 us
    all_to_all x2, blocking collectives, exchange(): lax.all_to_all(x, 'shard', split_axis=0, concat_axis=0, tiled=True, axis_...  23.8 us
    pallas_call x1, Pallas kernels, serve_step(): pl.pallas_call(merge_kernel, in_specs=[remote()] * 7, out_specs=[whole(),...  6.38 us
    all_to_all x1, starting transfers between devices, exchange(): lax.all_to_all(x, 'shard', split_axis=0, concat_axis=0, tiled=True, axis_...  5.54 us
    ppermute x3, starting transfers between devices, serve_step(): lax.ppermute(router, 'expert', [(z, z ^ k) for z in range(4)])  5.07 us
    ppermute x3, waiting for transfers between devices, serve_step(): lax.ppermute(router, 'expert', [(z, z ^ k) for z in range(4)])  4.91 us
    pallas_call x1, Pallas kernels, serve_step(): pl.pallas_call(unpack_kernel, in_specs=[whole()] * 6, out_specs=[remote()...  4.61 us
  transfers between devices with their start and end apart: 4, of which 3 were waited for; matrix products, arithmetic and copies ran while one was open for 0% of the time, Pallas kernels for 0%

profile of v6, /device:TPU:2, one launch (start us, length us, event | category | flops | bytes accessed | tf_op | source)
XLA Modules:
  0.0 103.2 jit_solution(18028110783192379391)
XLA Ops:
  0.6 6.4 %merge.1 = (f32[32,64,1024]{2,1,0:T(8,128)S(1)}, bf16[32,24,128]{2,1,0:T(8,128)(2,1)S(1)}) custom-call(f32[16]{0:T(128)} %shares.1, f32[16,64,1024]{2,1,0:T(8,128)} %a_gate.1, f32[16,64,1024]{2,1,0:T(8,128)} %b_gate.1, f32[16,64,1024]{2,1,0:T(8,128)} %a_up.1, f32[16,64,1024]{2,1,0:T(8,128)} %b_up.1, f32[16,64]{1,0:T(8,128)} %bitcast.5, f32[1,64]{1,0:T(1,128)} %bitcast.6), custom_call_target="tpu_custom_call" | custom-call | tf_op jit(solution)/shard_map/merge/pallas_call | solution.py:203
  7.0 13.3 %all_to_all.15.parts = bf16[32,24,128]{2,1,0:T(8,128)(2,1)S(1)} all-to-all(bf16[32,24,128]{2,1,0:T(8,128)(2,1)S(1)} %get-tuple-element.15), channel_id=1, replica_groups={{13,3,31,6,26,27,11,25,4,18,9,17,30,0,16,15,7,12,24,1,5,23,22,28,10,20,..., dimensions={0} | all-to-all | bytes 393216 | tf_op jit(solution)/shard_map/all_to_all | solution.py:197
  20.4 0.1 scale.1
  20.5 10.5 %all_to_all.16.scales = f32[32,8,128]{2,1,0:T(8,128)S(1)} all-to-all(f32[32,8,128]{2,1,0:T(8,128)S(1)} %get-tuple-element.16.spread), channel_id=1, replica_groups={{13,3,31,6,26,27,11,25,4,18,9,17,30,0,16,15,7,12,24,1,5,23,22,28,10,20,..., dimensions={0} | all-to-all | bytes 262144 | tf_op jit(solution)/shard_map/all_to_all | solution.py:197
  30.9 1.3 %pack.1 = bf16[32,512,128]{2,1,0:T(8,128)(2,1)S(1)} custom-call(f32[32,64,1024]{2,1,0:T(8,128)S(1)} %get-tuple-element.14.merged, f32[32,8,128]{2,1,0:T(8,128)S(1)} %all_to_all.16.scales), custom_call_target="tpu_custom_call" | custom-call | tf_op jit(solution)/shard_map/pack/pallas_call | solution.py:250
  32.2 0.0 copy-start
  32.2 2.0 %copy-done = bf16[32,512,128]{2,1,0:T(8,128)(2,1)} copy-done((bf16[32,512,128]{2,1,0:T(8,128)(2,1)}, bf16[32,512,128]{2,1,0:T(8,128)(2,1)S(1)}, u32[]{:S(2)}) %copy-start) | copy-done | bytes 4194328
  34.2 5.5 %all-to-all-start.2 = ((bf16[32,512,128]{2,1,0:T(8,128)(2,1)}), bf16[32,512,128]{2,1,0:T(8,128)(2,1)}, u32[]{:S(2)}, u32[]{:S(2)}) async-start(bf16[32,512,128]{2,1,0:T(8,128)(2,1)} %copy-done), calls=%async_computation.2 | async-start | bytes 8388608 | tf_op jit(solution)/shard_map/all_to_all | solution.py:197
  39.7 4.1 %collective-permute-start.2 = (bf16[16,2048]{1,0:T(8,128)(2,1)S(1)}, bf16[16,2048]{1,0:T(8,128)(2,1)S(1)}, u32[]{:S(2)}, u32[]{:S(2)}) collective-permute-start(bf16[16,2048]{1,0:T(8,128)(2,1)S(1)} %get-tuple-element.17.r0), channel_id=1, source_target_pairs={{0,96},{32,64},{64,32},{96,0},{1,97},{33,65},{65,33},{97,1},{2,98}... | collective-permute-start | bytes 196616 | tf_op jit(solution)/shard_map/ppermute | solution.py:245
  43.8 0.0 collective-permute-start.1
  43.8 0.9 collective-permute-start
  44.8 1.9 %collective-permute-done.2.r3 = bf16[16,2048]{1,0:T(8,128)(2,1)S(1)} collective-permute-done((bf16[16,2048]{1,0:T(8,128)(2,1)S(1)}, bf16[16,2048]{1,0:T(8,128)(2,1)S(1)}, u32[]{:S(2)}, u32[]{:S(2)}) %collective-permute-start.2) | collective-permute-done | bytes 65568 | tf_op jit(solution)/shard_map/ppermute | solution.py:245
  46.7 3.0 %collective-permute-done.1.r2 = bf16[16,2048]{1,0:T(8,128)(2,1)S(1)} collective-permute-done((bf16[16,2048]{1,0:T(8,128)(2,1)S(1)}, bf16[16,2048]{1,0:T(8,128)(2,1)S(1)}, u32[]{:S(2)}, u32[]{:S(2)}) %collective-permute-start.1) | collective-permute-done | bytes 65568 | tf_op jit(solution)/shard_map/ppermute | solution.py:245
  49.7 0.0 collective-permute-done.r1
  49.7 48.9 %all-to-all-done.2.arrived = bf16[32,512,128]{2,1,0:T(8,128)(2,1)} async-done(((bf16[32,512,128]{2,1,0:T(8,128)(2,1)}), bf16[32,512,128]{2,1,0:T(8,128)(2,1)}, u32[]{:S(2)}, u32[]{:S(2)}) %all-to-all-start.2) | async-done | bytes 4194336 | tf_op jit(solution)/shard_map/all_to_all | solution.py:197
  98.6 4.6 %unpack.1 = (bf16[16,32,2048]{2,1,0:T(8,128)(2,1)}, bf16[16,32,2048]{2,1,0:T(8,128)(2,1)}, bf16[64,2048]{1,0:T(8,128)(2,1)}, f32[16,32]{1,0:T(8,128)}, f32[16,32]{1,0:T(8,128)}) custom-call(bf16[32,512,128]{2,1,0:T(8,128)(2,1)} %all-to-all-done.2.arrived, f32[32,8,128]{2,1,0:T(8,128)S(1)} %get-tuple-element.16.spread, ...), custom_call_target="tpu_custom_call" | custom-call | tf_op jit(solution)/shard_map/unpack/pallas_call | solution.py:261
Async XLA Ops:
  32.2 2.0 %copy-start = (bf16[32,512,128]{2,1,0:T(8,128)(2,1)}, bf16[32,512,128]{2,1,0:T(8,128)(2,1)S(1)}, u32[]{:S(2)}) copy-start(bf16[32,512,128]{2,1,0:T(8,128)(2,1)S(1)} %pack.1) | copy-start | bytes 12582916
  34.2 64.4 %all-to-all-start.2 = ((bf16[32,512,128]{2,1,0:T(8,128)(2,1)}), bf16[32,512,128]{2,1,0:T(8,128)(2,1)}, u32[]{:S(2)}, u32[]{:S(2)}) async-start(bf16[32,512,128]{2,1,0:T(8,128)(2,1)} %copy-done), calls=%async_computation.2 | async-start | bytes 8388608 | tf_op jit(solution)/shard_map/all_to_all | solution.py:197
  39.7 7.0 %collective-permute-start.2 = (bf16[16,2048]{1,0:T(8,128)(2,1)S(1)}, bf16[16,2048]{1,0:T(8,128)(2,1)S(1)}, u32[]{:S(2)}, u32[]{:S(2)}) collective-permute-start(bf16[16,2048]{1,0:T(8,128)(2,1)S(1)} %get-tuple-element.17.r0), channel_id=1, source_target_pairs={{0,96},{32,64},{64,32},{96,0},{1,97},{33,65},{65,33},{97,1},{2,98}... | collective-permute-start | bytes 196616 | tf_op jit(solution)/shard_map/ppermute | solution.py:245
  43.8 5.9 %collective-permute-start.1 = (bf16[16,2048]{1,0:T(8,128)(2,1)S(1)}, bf16[16,2048]{1,0:T(8,128)(2,1)S(1)}, u32[]{:S(2)}, u32[]{:S(2)}) collective-permute-start(bf16[16,2048]{1,0:T(8,128)(2,1)S(1)} %get-tuple-element.17.r0), channel_id=1, source_target_pairs={{0,64},{32,96},{64,0},{96,32},{1,65},{33,97},{65,1},{97,33},{2,66}... | collective-permute-start | bytes 196616 | tf_op jit(solution)/shard_map/ppermute | solution.py:245
  43.8 5.9 %collective-permute-start = (bf16[16,2048]{1,0:T(8,128)(2,1)S(1)}, bf16[16,2048]{1,0:T(8,128)(2,1)S(1)}, u32[]{:S(2)}, u32[]{:S(2)}) collective-permute-start(bf16[16,2048]{1,0:T(8,128)(2,1)S(1)} %get-tuple-element.17.r0), channel_id=1, source_target_pairs={{0,32},{32,0},{64,96},{96,64},{1,33},{33,1},{65,97},{97,65},{2,34}... | collective-permute-start | bytes 196616 | tf_op jit(solution)/shard_map/ppermute | solution.py:245
